TPU v7x, 128 devices: a whole 4x4x4 slice. The times are simulated.
128 devices in a mesh: data: 128 (over z, y, x, core).
Axes of the slice: x: 4, y: 4, z: 4, core: 2. Of those that a mesh axis runs over, the one named last changes fastest.
Arguments:
- tokens: bfloat16 [262144, 512], P('data')
- w_in: bfloat16 [512, 2048], replicated
- w_out: bfloat16 [2048, 512], replicated
- task_heads: bfloat16 [6, 512, 3], replicated
- labels: int32 [6, 262144], P(None, 'data')
- label_mask: int32 [6, 262144], P(None, 'data')
Outputs:
- output 1: float32 [6], replicated
- output 2: float32 [1048576], P('data')
- output 3: float32 [1048576], P('data')
All inputs are finite; a program needn't handle non-finite values.
Results may differ from a plain program's by a relative error of at most 0.00315927.
Values are sent between devices in bfloat16 or wider.
A program may use at most 1 GiB of HBM per device.

v0:
```python
import jax
import jax.numpy as jnp
from jax import lax
from jax.sharding import PartitionSpec as P

SOLVER_STEPS = 20


def device_grads(x_loc, w_in, w_out, task_heads, lab_loc, mask_loc):
    pre_act = jnp.dot(x_loc, w_in, preferred_element_type=jnp.float32)
    act_out, gelu_slope = jax.jvp(jax.nn.gelu, (pre_act,), (jnp.ones_like(pre_act),))
    act_bf = act_out.astype(jnp.bfloat16)
    residual = x_loc.astype(jnp.float32) + jnp.dot(act_bf, w_out, preferred_element_type=jnp.float32)
    z_bf = residual.astype(jnp.bfloat16)
    logits = jnp.einsum("bd,tdc->tbc", z_bf, task_heads, preferred_element_type=jnp.float32)
    soft_prob = jax.nn.softmax(logits, axis=-1)
    class_ids = jnp.arange(logits.shape[-1])
    onehot = (lab_loc[:, :, None] == class_ids).astype(jnp.float32)
    d_logit = (mask_loc[:, :, None].astype(jnp.float32) * (soft_prob - onehot)).astype(jnp.bfloat16)
    d_resid = jnp.einsum("tbc,tdc->tbd", d_logit, task_heads, preferred_element_type=jnp.float32).astype(jnp.bfloat16)
    grad_w_out = jnp.einsum("bf,tbd->tfd", act_bf, d_resid, preferred_element_type=jnp.float32)
    d_act = jnp.einsum("tbd,fd->tbf", d_resid, w_out, preferred_element_type=jnp.float32)
    d_pre = (d_act * gelu_slope[None]).astype(jnp.bfloat16)
    grad_w_in = jnp.einsum("bd,tbf->tdf", x_loc, d_pre, preferred_element_type=jnp.float32)
    return grad_w_in, grad_w_out


def gram_of(grad_rows):
    return jnp.einsum("tk,sk->ts", grad_rows, grad_rows, precision=lax.Precision.HIGHEST, preferred_element_type=jnp.float32)


def solve_weights(gram_mat):
    num_tasks = gram_mat.shape[0]
    step_scale = jnp.trace(gram_mat) / num_tasks

    def solver_step(step_idx, weights):
        pull_vec = (gram_mat * weights[None, :]).sum(axis=1)
        raised = weights * jnp.exp(-pull_vec / step_scale)
        return raised / raised.sum()

    init_weights = jnp.full((num_tasks,), 1.0 / num_tasks, jnp.float32)
    return lax.fori_loop(0, SOLVER_STEPS, solver_step, init_weights)


def solution(mesh):
    group_size = mesh.shape["data"]

    def local_step(x_loc, w_in, w_out, task_heads, lab_loc, mask_loc):
        num_tasks = task_heads.shape[0]
        label_count = lax.psum(mask_loc.sum(axis=1), "data")
        inv_count = 1.0 / jnp.maximum(label_count, 1).astype(jnp.float32)
        grad_w_in, grad_w_out = device_grads(x_loc, w_in, w_out, task_heads, lab_loc, mask_loc)
        shards = []
        for grad_full in (grad_w_in, grad_w_out):
            scaled = (grad_full.reshape(num_tasks, group_size, -1) * inv_count[:, None, None]).astype(jnp.bfloat16)
            arrived = lax.all_to_all(scaled, "data", 1, 1, tiled=True)
            shards.append(arrived.sum(axis=1, dtype=jnp.float32))
        gram_mat = lax.psum(gram_of(shards[0]) + gram_of(shards[1]), "data")
        weights = solve_weights(gram_mat)
        grad_in = (weights[:, None] * shards[0]).sum(axis=0)
        grad_out = (weights[:, None] * shards[1]).sum(axis=0)
        return weights, grad_in, grad_out

    return jax.shard_map(local_step, mesh=mesh, in_specs=(P("data", None), P(), P(), P(), P(None, "data"), P(None, "data")), out_specs=(P(), P("data"), P("data")), check_vma=False)
```

profile of v0, /device:TPU:1, one launch (start us, length us, event | category | flops | bytes accessed | tf_op | source)
XLA Modules:
  0.0 974.6 jit_solution(3196922750218705989)
XLA Ops:
  0.6 1.7 fusion.24
  2.3 17.4 %fusion.13 = (f32[2048,2048]{1,0:T(8,128)}, f32[2048,2048]{1,0:T(8,128)}) fusion(bf16[2048,512]{1,0:T(8,128)(2,1)} %param.8, bf16[512,2048]{1,0:T(8,128)(2,1)S(1)} %copy-done), kind=kOutput, calls=%fused_computation.23 | convolution fusion | flops 4362076160 | bytes 37748736 | tf_op jit(solution)/shard_map/dot_general | solution.py:10
  19.7 10.4 %fusion.25 = (f32[6,2048]{1,0:T(8,128)S(1)}, f32[6,2048,3]{1,0,2:T(8,128)S(1)}) fusion(bf16[6,512,3]{1,2,0:T(4,128)(2,1)S(1)} %copy-done.4, bf16[2048,512]{1,0:T(8,128)(2,1)} %param.10, bf16[2048,512]{1,0:T(8,128)(2,1)} %param.8, f32[2048,2048]{1,0:T(8,128)} %get-tuple-element.60), kind=kOutput, calls=%fused_computation.48 | convolution fusion | flops 4373635072 | bytes 21186560 | tf_op jit(solution)/shard_map/bd,tdc->tbc/dot_general | solution.py:15
  30.3 3.7 convolution_convert_fusion
  34.1 4.5 copy-done.2
  38.5 34.3 %convolution_bitcast_fusion = f32[6,2048,512]{1,2,0:T(8,128)} fusion(bf16[6,2048,512]{2,1,0:T(8,128)(2,1)S(1)} %convolution_convert_fusion, f32[2048,2048]{1,0:T(8,128)} %get-tuple-element.60), kind=kOutput, calls=%fused_computation.26 | convolution fusion | flops 25807552512 | bytes 54525952 | tf_op jit(solution)/shard_map/bf,tbd->tfd/dot_general | solution.py:21
  72.8 24.6 %copy.33 = f32[6,2048,512]{2,1,0:T(8,128)} copy(f32[6,2048,512]{1,2,0:T(8,128)} %convolution_bitcast_fusion) | data formatting | bytes 50331648 | tf_op jit(solution)/shard_map/bf,tbd->tfd/transpose | solution.py:21
  97.5 27.2 %reshape.22 = f32[6,128,8192]{2,1,0:T(8,128)} reshape(f32[6,2048,512]{2,1,0:T(8,128)} %copy.33) | data formatting | bytes 50331648 | tf_op jit(solution)/shard_map/reshape | solution.py:55
  124.7 61.2 %fusion.14 = f32[6,512,2048]{1,2,0:T(8,128)} fusion(f32[2048,2048]{1,0:T(8,128)} %get-tuple-element.59, bf16[6,2048,512]{2,1,0:T(8,128)(2,1)} %copy-done.2, bf16[2048,512]{1,0:T(8,128)(2,1)} %param.8, bf16[2048,512]{1,0:T(8,128)(2,1)S(1)} %copy-done.7), kind=kOutput, calls=%fused_computation.25 | convolution fusion | flops 51589939200 | bytes 58720256 | tf_op jit(solution)/shard_map/bd,tbf->tdf/dot_general | solution.py:24
  185.9 25.0 %copy.30 = f32[6,512,2048]{2,1,0:T(8,128)} copy(f32[6,512,2048]{1,2,0:T(8,128)} %fusion.14) | data formatting | bytes 50331648 | tf_op jit(solution)/shard_map/bd,tbf->tdf/transpose | solution.py:24
  210.9 30.2 %reshape.21 = f32[6,128,8192]{2,1,0:T(8,128)} reshape(f32[6,512,2048]{2,1,0:T(8,128)} %copy.30) | data formatting | bytes 50331648 | tf_op jit(solution)/shard_map/reshape | solution.py:55
  241.1 68.9 %psum.14 = s32[6]{0:T(128)S(1)} all-reduce(s32[6]{0:T(128)S(1)} %copy-done.6), channel_id=1, replica_groups=mesh['data'=128] {'data'}, use_global_device_ids=true, to_apply=%region_3.0 | all-reduce | flops 6 | bytes 48 | tf_op jit(solution)/shard_map/psum | solution.py:50
  310.0 21.3 %multiply_convert_fusion.2 = (bf16[6,128,8192]{2,1,0:T(8,128)(2,1)}, bf16[6,128,8192]{2,1,0:T(8,128)(2,1)S(1)}) fusion(f32[6,128,8192]{2,1,0:T(8,128)} %reshape.22, f32[6]{0:T(128)S(1)} %convert_divide_fusion, f32[6,128,8192]{2,1,0:T(8,128)} %reshape.21), kind=kLoop, calls=%fused_computation.9 | loop fusion | flops 25165824 | bytes 75497496 | tf_op jit(solution)/shard_map/convert_element_type | solution.py:55
  331.3 25.8 %copy.31 = bf16[6,128,8192]{2,0,1:T(8,128)(2,1)} copy(bf16[6,128,8192]{2,1,0:T(8,128)(2,1)S(1)} %get-tuple-element.56) | data formatting | bytes 25165824 | tf_op jit(solution)/shard_map/convert_element_type | solution.py:55
  357.1 5.7 all-to-all-start
  362.7 13.8 %copy.34 = bf16[6,128,8192]{2,0,1:T(8,128)(2,1)} copy(bf16[6,128,8192]{2,1,0:T(8,128)(2,1)} %get-tuple-element.55) | data formatting | bytes 25165824 | tf_op jit(solution)/shard_map/convert_element_type | solution.py:55
  376.5 216.1 %all-to-all-done = bf16[6,128,8192]{2,0,1:T(8,128)(2,1)} async-done(((bf16[6,128,8192]{2,0,1:T(8,128)(2,1)}), bf16[6,128,8192]{2,0,1:T(8,128)(2,1)}, u32[]{:S(2)}, u32[]{:S(2)}) %all-to-all-start) | async-done | bytes 12582944 | tf_op jit(solution)/shard_map/all_to_all | solution.py:56
  592.6 28.0 %all-to-all-start.1 = ((bf16[6,128,8192]{2,0,1:T(8,128)(2,1)}), bf16[6,128,8192]{2,0,1:T(8,128)(2,1)}, u32[]{:S(2)}, u32[]{:S(2)}) async-start(bf16[6,128,8192]{2,0,1:T(8,128)(2,1)} %copy.34), calls=%async_computation.1 | async-start | bytes 33554432 | tf_op jit(solution)/shard_map/all_to_all | solution.py:56
  620.7 7.3 convert_reduce_fusion.1
  628.0 0.7 fusion.26
  628.7 221.8 %all-to-all-done.1 = bf16[6,128,8192]{2,0,1:T(8,128)(2,1)} async-done(((bf16[6,128,8192]{2,0,1:T(8,128)(2,1)}), bf16[6,128,8192]{2,0,1:T(8,128)(2,1)}, u32[]{:S(2)}, u32[]{:S(2)}) %all-to-all-start.1) | async-done | bytes 12582944 | tf_op jit(solution)/shard_map/all_to_all | solution.py:56
  850.5 7.2 convert_reduce_fusion
  857.6 0.7 convolution_add_fusion
  858.3 85.8 %psum.15 = f32[6,6]{1,0:T(8,128)S(1)} all-reduce(f32[6,6]{1,0:T(8,128)S(1)} %convolution_add_fusion), channel_id=1, replica_groups=mesh['data'=128] {'data'}, use_global_device_ids=true, to_apply=%region_6.0 | all-reduce | flops 36 | bytes 288 | tf_op jit(solution)/shard_map/psum | solution.py:58
  945.3 28.4 %while.11 = (s32[]{:T(128)}, f32[6]{0:T(128)S(1)}, f32[6,6]{1,0:T(8,128)S(1)}, f32[]{:T(128)}, s32[]{:T(128)}, /*index=5*/s32[]{:T(128)}) while((s32[]{:T(128)}, f32[6]{0:T(128)S(1)}, f32[6,6]{1,0:T(8,128)S(1)}, f32[]{:T(128)}, s32[]{:T(128)}, /*index=5*/s32[]{:T(128)}) %tuple.34), condition=%wide.region_11.12_spmd.clone, body=%wide.region_8.11_spmd.clone.sunk | while | flops 110 | bytes 452 | solution.py:42
  946.1 0.6 broadcast_divide_fusion.2
  947.5 0.6 broadcast_divide_fusion.2
  948.9 0.6 broadcast_divide_fusion.2
  950.3 0.6 broadcast_divide_fusion.2
  951.8 0.6 broadcast_divide_fusion.2
  954.6 0.6 broadcast_divide_fusion.2
  973.7 0.8 multiply_reduce_fusion.1
  (94 shorter events, 24.6 us)
Async XLA Ops:
  0.6 1.7 copy-start
  2.3 17.4 %copy-start.4 = (bf16[6,512,3]{1,2,0:T(4,128)(2,1)S(1)}, bf16[6,512,3]{1,2,0:T(4,128)(2,1)}, u32[]{:S(2)}) copy-start(bf16[6,512,3]{1,2,0:T(4,128)(2,1)} %param.11) | copy-start | bytes 55300
  19.7 10.5 %copy-start.3 = (s32[6,2048]{1,0:T(8,128)S(1)}, s32[6,2048]{1,0:T(8,128)}, u32[]{:S(2)}) copy-start(s32[6,2048]{1,0:T(8,128)} %param.12) | copy-start | bytes 147460
  34.0 4.5 copy-start.2
  97.5 27.2 %copy-start.7 = (bf16[2048,512]{1,0:T(8,128)(2,1)S(1)}, bf16[2048,512]{1,0:T(8,128)(2,1)}, u32[]{:S(2)}) copy-start(bf16[2048,512]{1,0:T(8,128)(2,1)} %param.10) | copy-start | bytes 6291460
  210.9 30.2 %copy-start.6 = (s32[6]{0:T(128)S(1)}, s32[6]{0:T(128)}, u32[]{:S(2)}) copy-start(s32[6]{0:T(128)} %get-tuple-element.53) | copy-start | bytes 76
  357.1 235.6 %all-to-all-start = ((bf16[6,128,8192]{2,0,1:T(8,128)(2,1)}), bf16[6,128,8192]{2,0,1:T(8,128)(2,1)}, u32[]{:S(2)}, u32[]{:S(2)}) async-start(bf16[6,128,8192]{2,0,1:T(8,128)(2,1)} %copy.31), calls=%async_computation | async-start | bytes 33554432 | tf_op jit(solution)/shard_map/all_to_all | solution.py:56
  592.6 257.8 %all-to-all-start.1 = ((bf16[6,128,8192]{2,0,1:T(8,128)(2,1)}), bf16[6,128,8192]{2,0,1:T(8,128)(2,1)}, u32[]{:S(2)}, u32[]{:S(2)}) async-start(bf16[6,128,8192]{2,0,1:T(8,128)(2,1)} %copy.34), calls=%async_computation.1 | async-start | bytes 33554432 | tf_op jit(solution)/shard_map/all_to_all | solution.py:56
  620.7 353.9 %copy-start.1 = (bf16[512,2048]{1,0:T(8,128)(2,1)S(1)}, bf16[512,2048]{1,0:T(8,128)(2,1)}, u32[]{:S(2)}) copy-start(bf16[512,2048]{1,0:T(8,128)(2,1)} %param.9) | copy-start | bytes 6291460
  973.7 0.9 copy-start.5
where the time goes:
time: 977 us; the launch traced here: 975 us
  waiting for transfers between devices  438 us (45%)
  blocking collectives  155 us (16%)
  local copies, waits for them, and re-layouts  151 us (15%)
  matrix products  128 us (13%)
  other arithmetic  66.7 us (7%)
  starting transfers between devices  33.7 us (3%)
    all_to_all x2, waiting for transfers between devices, local_step(): arrived = lax.all_to_all(scaled, 'data', 1, 1, tiled=True)  438 us
    psum x1, blocking collectives, local_step(): gram_mat = lax.psum(gram_of(shards[0]) + gram_of(shards[1]), 'data')  85.8 us
    psum x1, blocking collectives, local_step(): label_count = lax.psum(mask_loc.sum(axis=1), 'data')  68.9 us
    dot_general x1, matrix products, device_grads(): jnp.einsum('bd,tbf->tdf', x_loc, d_pre, preferred_element_type=jnp.float32)  61.2 us
    reshape x2, local copies, waits for them, and re-layouts, local_step(): grad_full.reshape(num_tasks, group_size, -1) * inv_count[:, None, None]  57.4 us
    convert_element_type x2, local copies, waits for them, and re-layouts, local_step(): (grad_full.reshape(num_tasks, group_size, -1) * inv_count[:, None, None])...  39.5 us
    dot_general x1, matrix products, device_grads(): jnp.einsum('bf,tbd->tfd', act_bf, d_resid, preferred_element_type=jnp.flo...  34.3 us
    all_to_all x2, starting transfers between devices, local_step(): arrived = lax.all_to_all(scaled, 'data', 1, 1, tiled=True)  33.7 us
  transfers between devices with their start and end apart: 2, of which 2 were waited for; matrix products, arithmetic and copies ran while one was open for 2% of the time, Pallas kernels for 0%

commit v1 on v0

v1 whole, which is shorter than its diff:
```python
import functools

import jax
import jax.numpy as jnp
from jax import lax
from jax.experimental import pallas as pl
from jax.experimental.pallas import tpu as pltpu
from jax.sharding import PartitionSpec as P

SOLVER_STEPS = 20
T = 6
MESH = pl.DeviceIdType.MESH
STRIDES = (32, 8, 2)
RING, DEPTH, XRING = 8, 4, 3
F32, BF16 = jnp.float32, jnp.bfloat16


def perm(order, z, y, x):
    return ((z, y, x), (y, x, z), (x, z, y))[order]


def kernel(rb_count, cnt_ref, aT_hbm, xT_hbm, dz_hbm, w2T_hbm, gp_hbm,
           alpha_ref, out1_ref, out2_ref,
           aT, xT, dz, w2T, gp, q, inv, hb, xr, dbuf, ebuf, fbuf, r1, r2, r3, shard, gb, ar_s, ar_r,
           ld_sem, gp_sem, xs_sem, xr_sem, s_sem, r_sem, ars_sem, arr_sem, gs_sem, gr_sem):
    nchunk = 4 * rb_count
    nfb = 2 * rb_count
    me = lax.axis_index("data")
    core = lax.rem(me, 2)
    coord = (lax.div(me, 32), lax.rem(lax.div(me, 8), 4), lax.rem(lax.div(me, 2), 4))
    partner = me + 1 - 2 * core

    def nb(dim, step):
        u = coord[dim]
        return (me + (lax.rem(u + step + 4, 4) - u) * STRIDES[dim],)

    def rel(dim, step):
        return lax.rem(coord[dim] + step + 4, 4)

    loads = [pltpu.make_async_copy(aT_hbm.at[i], aT.at[i], ld_sem.at[i]) for i in range(rb_count)]
    dz_loads = [pltpu.make_async_copy(dz_hbm.at[t], dz.at[t], ld_sem.at[rb_count + t]) for t in range(T)]
    x_load = pltpu.make_async_copy(xT_hbm, xT, ld_sem.at[rb_count + T])
    w_load = pltpu.make_async_copy(w2T_hbm, w2T, ld_sem.at[rb_count + T + 1])

    def gp_load(fb):
        cols = pl.ds(pl.multiple_of(fb * 256, 256), 256)
        return pltpu.make_async_copy(gp_hbm.at[:, cols], gp.at[lax.rem(fb, 2)], gp_sem.at[lax.rem(fb, 2)])

    loads[0].start()
    for c in dz_loads:
        c.start()
    w_load.start()
    x_load.start()
    gp_load(0).start()
    for c in loads[1:]:
        c.start()

    barrier = pltpu.get_barrier_semaphore()
    peers = [(partner,)] + [nb(d, s) for d in range(3) for s in (1, -1)]
    for p in peers:
        pl.semaphore_signal(barrier, inc=1, device_id=p, device_id_type=MESH)
    pl.semaphore_wait(barrier, 7)

    def all_reduce(base, val):
        plist = [(partner,)]
        for d in range(3):
            odd = lax.rem(coord[d], 2)
            plist.append(nb(d, 1 - 2 * odd))
            plist.append(nb(d, 2 * odd - 1))
        for i, p in enumerate(plist):
            s = base + i
            ar_s[s] = val
            cp = pltpu.make_async_remote_copy(
                src_ref=ar_s.at[s], dst_ref=ar_r.at[s], send_sem=ars_sem.at[s], recv_sem=arr_sem.at[s],
                device_id=p, device_id_type=MESH)
            cp.start()
            cp.wait()
            val = val + ar_r[s]
        return val

    total = all_reduce(0, cnt_ref[...])
    inv_all = 1.0 / jnp.maximum(total, 1.0)
    for t in range(T):
        inv[t] = jnp.broadcast_to(inv_all[t:t + 1, :], (8, 128))

    srcs = (dbuf, ebuf, fbuf)
    recvs = (r1, r2, r3)

    def dims_of(p, t):
        return (t % 3 + p) % 3, (1 if t < 3 else -1)

    def drain_sends(p, d):
        ref = recvs[p].at[0]
        pltpu.make_async_copy(ref, ref, s_sem.at[p, d]).wait()

    def send(p, k, t, blk, kind, step, dim):
        slot, d = lax.rem(k, RING), lax.rem(k, DEPTH)
        pltpu.make_async_remote_copy(
            src_ref=srcs[p].at[d, t, blk], dst_ref=recvs[p].at[slot, kind, t],
            send_sem=s_sem.at[p, d], recv_sem=r_sem.at[p, 0 if kind == 0 else 1, slot],
            device_id=nb(dim, step), device_id_type=MESH).start()

    def open_phase(p, k):
        for t in range(T):
            dim, sg = dims_of(p, t)
            send(p, k, t, rel(dim, 2), 0, sg, dim)
        for t in range(T):
            dim, sg = dims_of(p, t)
            send(p, k, t, rel(dim, -sg), 1, -sg, dim)

    def relay(p, k):
        slot, d = lax.rem(k, RING), lax.rem(k, DEPTH)
        ref = recvs[p].at[slot, 0]
        pltpu.make_async_copy(ref, ref, r_sem.at[p, 0, slot]).wait()
        for t in range(T):
            dim, sg = dims_of(p, t)
            v = rel(dim, sg)
            srcs[p][d, t, v] = srcs[p][d, t, v] + recvs[p][slot, 0, t]
        for t in range(T):
            dim, sg = dims_of(p, t)
            send(p, k, t, rel(dim, sg), 2, sg, dim)

    def close(p, k):
        slot, d = lax.rem(k, RING), lax.rem(k, DEPTH)
        ref = recvs[p].at[slot, pl.ds(1, 2)]
        pltpu.make_async_copy(ref, ref, r_sem.at[p, 1, slot]).wait()
        if p < 2:
            @pl.when(k >= DEPTH)
            def _():
                drain_sends(p + 1, d)
        for t in range(T):
            dim, _ = dims_of(p, t)
            out = srcs[p][d, t, coord[dim]] + recvs[p][slot, 1, t] + recvs[p][slot, 2, t]
            if p < 2:
                srcs[p + 1][d, t] = out
            else:
                shard[t, k] = out
        if p < 2:
            open_phase(p + 1, k)

    def half_copy(k, half):
        hs, xs = lax.rem(k, 2), lax.rem(k, XRING)
        return pltpu.make_async_remote_copy(
            src_ref=hb.at[hs, 1 - core, pl.ds(3 * half, 3)], dst_ref=xr.at[xs, pl.ds(3 * half, 3)],
            send_sem=xs_sem.at[hs, half], recv_sem=xr_sem.at[xs, half],
            device_id=(partner,), device_id_type=MESH)

    def merge(k):
        d, hs, xs = lax.rem(k, DEPTH), lax.rem(k, 2), lax.rem(k, XRING)
        half_copy(k, 0).wait_recv()
        half_copy(k, 1).wait_recv()

        @pl.when(k >= DEPTH)
        def _():
            drain_sends(0, d)
        for t in range(T):
            for pair in range(32):
                rows = slice(16 * pair, 16 * pair + 16)
                s = hb[hs, core, t, rows, :].astype(F32) + xr[xs, t, rows, :].astype(F32)
                for e in range(2):
                    i = 2 * pair + e
                    a, b, c = perm(t % 3, i // 16, (i // 4) % 4, i % 4)
                    dbuf[d, t, a, b, c] = s[8 * e:8 * e + 8]
        open_phase(0, k)

    def emit(hs, t, acc):
        row = inv[t][0:1, :]
        hb[hs, 0, t] = (acc[:, :128] * row).astype(BF16)
        hb[hs, 1, t] = (acc[:, 128:] * row).astype(BF16)

    def compute_out(k, half):
        j = lax.div(k, 2)
        rb, cb = lax.div(j, 2), lax.rem(j, 2)
        hs = lax.rem(k, 2)
        cols = pl.ds(pl.multiple_of(cb * 256, 256), 256)
        if half == 0:
            for i in range(rb_count):
                @pl.when(j == 2 * i)
                def _():
                    loads[i].wait()

        @pl.when(k == 0)
        def _():
            for t in range(3):
                dz_loads[3 * half + t].wait()

        def task(t, _):
            acc = jnp.dot(aT[rb], dz[t, :, cols], preferred_element_type=F32)
            emit(hs, t, acc)
            return 0
        lax.fori_loop(3 * half, 3 * half + 3, task, 0)

    def compute_in(k, half):
        fb = lax.div(k, 2)
        hs, gs = lax.rem(k, 2), lax.rem(fb, 2)
        if half == 0:
            @pl.when(k == 1)
            def _():
                w_load.wait()
                x_load.wait()
            gp_load(fb).wait()

            @pl.when(fb + 1 < nfb)
            def _():
                gp_load(fb + 1).start()
        tok = q.shape[0]
        step = tok // 4

        def task(t, _):
            def tile(i, _):
                rows = pl.ds(pl.multiple_of(i * step, step), step)
                d_act = jnp.dot(dz[t, rows, :], w2T[fb], preferred_element_type=F32)
                q[rows, :] = (d_act * gp[gs, rows, :]).astype(BF16)
                return 0
            lax.fori_loop(0, 4, tile, 0)
            acc = jnp.dot(xT[...], q[...], preferred_element_type=F32)
            emit(hs, t, acc)
            return 0
        lax.fori_loop(3 * half, 3 * half + 3, task, 0)

    def compute(k, half):
        @pl.when(k < nchunk)
        def _():
            if half == 0:
                @pl.when(k >= 2)
                def _():
                    half_copy(k, 0).wait_send()
                    half_copy(k, 1).wait_send()

            @pl.when(lax.rem(k, 2) == 0)
            def _():
                compute_out(k, half)

            @pl.when(lax.rem(k, 2) == 1)
            def _():
                compute_in(k, half)
            half_copy(k, half).start()

    def at(k, fn):
        @pl.when((k >= 0) & (k < nchunk))
        def _():
            fn(k)

    def slot(kk, _):
        at(kk - 3, functools.partial(relay, 0))
        at(kk - 6, functools.partial(relay, 1))
        at(kk - 9, functools.partial(relay, 2))
        compute(kk, 0)
        at(kk - 1, merge)
        at(kk - 4, functools.partial(close, 0))
        at(kk - 7, functools.partial(close, 1))
        at(kk - 10, functools.partial(close, 2))
        compute(kk, 1)
        return 0
    lax.fori_loop(0, nchunk + 10, slot, 0)

    for i in range(DEPTH):
        for p in range(3):
            drain_sends(p, i)
    for k in (nchunk - 2, nchunk - 1):
        half_copy(k, 0).wait_send()
        half_copy(k, 1).wait_send()

    pairs = [(t, s) for t in range(T) for s in range(t, T)]

    def gram_step(k, accs):
        rows = [shard[t, k] for t in range(T)]
        return tuple(acc + rows[t] * rows[s] for acc, (t, s) in zip(accs, pairs))
    accs = lax.fori_loop(0, nchunk, gram_step, tuple(jnp.zeros((8, 128), F32) for _ in pairs))
    row_id = lax.broadcasted_iota(jnp.int32, (8, 128), 0)
    col_id = lax.broadcasted_iota(jnp.int32, (8, 128), 1)
    gram = jnp.zeros((8, 128), F32)
    for acc, (t, s) in zip(accs, pairs):
        val = jnp.sum(jnp.sum(acc, axis=0, keepdims=True), axis=1, keepdims=True)
        hit = ((row_id == t) & (col_id == s)) | ((row_id == s) & (col_id == t))
        gram = jnp.where(hit, val, gram)
    gram = all_reduce(7, gram)

    diag = jnp.where(row_id == col_id, gram, 0.0)
    scale = jnp.sum(jnp.sum(diag, axis=0, keepdims=True), axis=1, keepdims=True) / T
    w_row = jnp.where(col_id[0:1, :] < T, jnp.full((1, 128), 1.0 / T, F32), 0.0)
    w_col = jnp.where(row_id[:, 0:1] < T, jnp.full((8, 1), 1.0 / T, F32), 0.0)

    def solver(_, carry):
        wr, wc = carry
        pull_c = jnp.sum(gram * wr, axis=1, keepdims=True)
        pull_r = jnp.sum(gram * wc, axis=0, keepdims=True)
        rc = wc * jnp.exp(-pull_c / scale)
        rr = wr * jnp.exp(-pull_r / scale)
        return rr / jnp.sum(rr, axis=1, keepdims=True), rc / jnp.sum(rc, axis=0, keepdims=True)
    w_row, w_col = lax.fori_loop(0, SOLVER_STEPS, solver, (w_row, w_col))
    alpha_ref[...] = jnp.broadcast_to(w_row, (8, 128))

    alphas = [jnp.broadcast_to(w_col[t:t + 1, :], (8, 128)) for t in range(T)]

    def combine(k, _):
        tot = alphas[0] * shard[0, k]
        for t in range(1, T):
            tot = tot + alphas[t] * shard[t, k]
        gb[core, k] = tot
        return 0
    lax.fori_loop(0, nchunk, combine, 0)
    swap = pltpu.make_async_remote_copy(
        src_ref=gb.at[core], dst_ref=gb.at[core], send_sem=gs_sem, recv_sem=gr_sem,
        device_id=(partner,), device_id_type=MESH)
    swap.start()
    swap.wait()
    for h in range(2):
        for fb in range(nfb):
            tile = gb[h, 2 * fb + 1]
            rows = jnp.where(core == 0, tile[0:4], tile[4:8])
            for r in range(4):
                o = r * 2 * nfb + 2 * fb + h
                out1_ref[o:o + 1, :] = rows[r:r + 1]
        for rbl in range(rb_count // 2):
            for cb in range(2):
                tile = gb[h, 4 * ((rb_count // 2) * core + rbl) + 2 * cb]
                for r in range(8):
                    o = (8 * rbl + r) * 4 + 2 * cb + h
                    out2_ref[o:o + 1, :] = tile[r:r + 1]


def reduce_and_solve(cnt, aT, xT, dz, w2T, gp):
    rb, _, tok = aT.shape
    nchunk = 4 * rb
    any_spec = pl.BlockSpec(memory_space=pl.ANY)
    vm = pl.BlockSpec(memory_space=pltpu.VMEM)
    rows = 4 * rb * 512 // 128
    V = pltpu.VMEM
    DS = pltpu.SemaphoreType.DMA
    return pl.pallas_call(
        functools.partial(kernel, rb),
        name="grads_rs",
        out_shape=[jax.ShapeDtypeStruct((8, 128), F32), jax.ShapeDtypeStruct((rows, 128), F32), jax.ShapeDtypeStruct((rows, 128), F32)],
        in_specs=[vm] + [any_spec] * 5,
        out_specs=[vm] * 3,
        scratch_shapes=[
            V((rb, 512, tok), BF16), V((512, tok), BF16), V((T, tok, 512), BF16), V((2 * rb, 512, 256), BF16),
            V((2, tok, 256), F32), V((tok, 256), BF16), V((T, 8, 128), F32),
            V((2, 2, T, 512, 128), BF16), V((XRING, T, 512, 128), BF16),
            V((DEPTH, T, 4, 4, 4, 8, 128), F32), V((DEPTH, T, 4, 4, 8, 128), F32), V((DEPTH, T, 4, 8, 128), F32),
            V((RING, 3, T, 4, 4, 8, 128), F32), V((RING, 3, T, 4, 8, 128), F32), V((RING, 3, T, 8, 128), F32),
            V((T, nchunk, 8, 128), F32), V((2, nchunk, 8, 128), F32), V((14, 8, 128), F32), V((14, 8, 128), F32),
            DS((rb + T + 2,)), DS((2,)), DS((2, 2)), DS((XRING, 2)), DS((3, DEPTH)), DS((3, 2, RING)),
            DS((14,)), DS((14,)), DS, DS,
        ],
        compiler_params=pltpu.CompilerParams(collective_id=0, has_side_effects=True, vmem_limit_bytes=66 * 1000 * 1000),
    )(cnt, aT, xT, dz, w2T, gp)


def forward(x_loc, w_in, w_out, task_heads, lab_loc, mask_loc):
    pre_act = jnp.dot(x_loc, w_in, preferred_element_type=F32)
    act_out, gelu_slope = jax.jvp(jax.nn.gelu, (pre_act,), (jnp.ones_like(pre_act),))
    act_bf = act_out.astype(BF16)
    residual = x_loc.astype(F32) + jnp.dot(act_bf, w_out, preferred_element_type=F32)
    z_bf = residual.astype(BF16)
    logits = jnp.einsum("bd,tdc->tbc", z_bf, task_heads, preferred_element_type=F32)
    soft_prob = jax.nn.softmax(logits, axis=-1)
    onehot = (lab_loc[:, :, None] == jnp.arange(logits.shape[-1])).astype(F32)
    d_logit = (mask_loc[:, :, None].astype(F32) * (soft_prob - onehot)).astype(BF16)
    d_resid = jnp.einsum("tbc,tdc->tbd", d_logit, task_heads, preferred_element_type=F32).astype(BF16)
    return act_bf, gelu_slope, d_resid


def solution(mesh):
    def local_step(x_loc, w_in, w_out, task_heads, lab_loc, mask_loc):
        tok = x_loc.shape[0]
        hid = w_in.shape[1]
        rb = hid // 512
        cnt = mask_loc.sum(axis=1).astype(F32)
        cnt = jnp.broadcast_to(jnp.pad(cnt, (0, 2))[:, None], (8, 128))
        act, slope, dz = forward(x_loc, w_in, w_out, task_heads, lab_loc, mask_loc)
        aT = act.reshape(tok, 64, rb, 8).transpose(2, 1, 3, 0).reshape(rb, 512, tok)
        w2T = w_out.reshape(2 * rb, 256, 512).transpose(0, 2, 1)
        alpha, g_in, g_out = reduce_and_solve(cnt, aT, x_loc.T, dz, w2T, slope)
        return alpha[0, :6], g_in.reshape(-1), g_out.reshape(-1)

    return jax.shard_map(local_step, mesh=mesh, in_specs=(P("data", None), P(), P(), P(), P(None, "data"), P(None, "data")), out_specs=(P(), P("data"), P("data")), check_vma=False)
```

time: 977 us -> 274 us (0.28)
  waiting for transfers between devices: 438 us -> 0 us
  Pallas kernels: 0 us -> 207 us
  blocking collectives: 155 us -> 0 us
  local copies, waits for them, and re-layouts: 151 us -> 30.2 us
  matrix products: 128 us -> 33.4 us
  other arithmetic: 66.7 us -> 1.16 us
  starting transfers between devices: 33.7 us -> 0 us
    all_to_all x2 -> x0, waiting for transfers between devices: 438 us -> none  [local_step(): arrived = lax.all_to_all(scaled, 'data', 1, 1, tiled=True)]
    pallas_call x0 -> x1, Pallas kernels: none -> 207 us  [reduce_and_solve(): pl.pallas_call(functools.partial(kernel, rb), name='grads_rs', out_shape=...]
    psum x2 -> x0, blocking collectives: 155 us -> none  [the longest x1 85.8 us: local_step(): gram_mat = lax.psum(gram_of(shards[0]) + gram_of(shards[1]), 'data')]
    dot_general x7 -> x3, matrix products: 128 us -> 33.4 us  [the longest x1 19 us: forward(): pre_act = jnp.dot(x_loc, w_in, preferred_element_type=F32)]
    reshape x2 -> x1, local copies, waits for them, and re-layouts: 57.4 us -> 2.42 us  [local_step(): w2T = w_out.reshape(2 * rb, 256, 512).transpose(0, 2, 1)]
    transpose x2 -> x1, local copies, waits for them, and re-layouts: 49.6 us -> 8.41 us  [local_step(): aT = act.reshape(tok, 64, rb, 8).transpose(2, 1, 3, 0).reshape(rb, 512, tok)]
    all_to_all x2 -> x0, starting transfers between devices: 33.7 us -> none  [local_step(): arrived = lax.all_to_all(scaled, 'data', 1, 1, tiled=True)]
    reduce_sum x46 -> x1, other arithmetic: 32.3 us -> 0.04 us  [forward(): soft_prob = jax.nn.softmax(logits, axis=-1)]
  transfers between devices with their start and end apart: 2 -> 0, of which waited for: 2 -> 0; matrix products, arithmetic and copies ran while one was open for 2% -> 0% of each run, Pallas kernels for 0% -> 0%
where the time goes in v1:
time: 274 us; the launch traced here: 273 us
  Pallas kernels  207 us (76%)
  matrix products  33.4 us (12%)
  local copies, waits for them, and re-layouts  30.2 us (11%)
    pallas_call x1, Pallas kernels, reduce_and_solve(): pl.pallas_call(functools.partial(kernel, rb), name='grads_rs', out_shape=...  207 us
    dot_general x1, matrix products, forward(): pre_act = jnp.dot(x_loc, w_in, preferred_element_type=F32)  19 us
    convert_element_type x1, local copies, waits for them, and re-layouts, forward(): act_bf = act_out.astype(BF16)  12.3 us
    transpose x1, local copies, waits for them, and re-layouts, local_step(): aT = act.reshape(tok, 64, rb, 8).transpose(2, 1, 3, 0).reshape(rb, 512, tok)  8.41 us
    dot_general x1, matrix products, forward(): jnp.einsum('bd,tdc->tbc', z_bf, task_heads, preferred_element_type=F32)  7.99 us
    dot_general x1, matrix products, forward(): jnp.einsum('tbc,tdc->tbd', d_logit, task_heads, preferred_element_type=F32)  6.38 us

profile of v1, /device:TPU:1, one launch (start us, length us, event | category | flops | bytes accessed | tf_op | source)
XLA Modules:
  0.0 272.9 jit_solution(17699054767000017377)
XLA Ops:
  0.6 0.0 copy-start
  0.6 1.0 fusion.14
  1.7 0.7 broadcast_in_dim.2.cnt_ref
  2.4 19.0 %fusion.9 = (f32[2048,2048]{1,0:T(8,128)}, bf16[2048,2048]{1,0:T(8,128)(2,1)}) fusion(bf16[2048,512]{1,0:T(8,128)(2,1)} %param.6, bf16[512,2048]{1,0:T(8,128)(2,1)} %param.7), kind=kOutput, calls=%fused_computation.11 | convolution fusion | flops 4370464768 | bytes 29360128 | tf_op jit(solution)/shard_map/dot_general | solution.py:352
  21.4 12.3 %copy.24 = bf16[2048,2048]{0,1:T(8,128)(2,1)} copy(bf16[2048,2048]{1,0:T(8,128)(2,1)} %get-tuple-element.10) | data formatting | bytes 16777216 | tf_op jit(solution)/shard_map/convert_element_type | solution.py:354
  33.7 0.0 copy-start.1
  33.7 8.4 %copy.39 = bf16[4,64,8,2048]{3,2,1,0:T(8,128)(2,1)} copy(bf16[4,64,8,2048]{3,2,0,1:T(8,128)(2,1)} %bitcast.26) | data formatting | bytes 16777216 | tf_op jit(solution)/shard_map/transpose | solution.py:373
  42.1 0.0 copy-done.1
  42.1 2.4 copy.26
  44.6 0.0 copy-done
  44.6 0.0 copy-start.3
  44.6 8.0 %fusion.15 = (f32[6,2048]{1,0:T(8,128)S(1)}, f32[6,2048,3]{1,0,2:T(8,128)S(1)}) fusion(bf16[6,512,3]{1,2,0:T(4,128)(2,1)S(1)} %copy-done, bf16[2048,2048]{1,0:T(8,128)(2,1)} %get-tuple-element.10, bf16[2048,512]{1,0:T(8,128)(2,1)} %param.8, bf16[2048,512]{1,0:T(8,128)(2,1)S(1)} %copy-done.1), kind=kOutput, calls=%fused_computation.26 | convolution fusion | flops 4335886336 | bytes 12797952 | tf_op jit(solution)/shard_map/bd,tdc->tbc/dot_general | solution.py:357
  52.6 0.0 copy-start.2
  52.7 0.0 copy-done.3
  52.7 0.1 multiply_convert_fusion.1
  52.7 6.4 %convolution_convert_fusion.dz_hbm = bf16[6,2048,512]{2,1,0:T(8,128)(2,1)} fusion(bf16[6,512,3]{1,2,0:T(4,128)(2,1)S(1)} %copy-done, bf16[6,2048,3]{1,0,2:T(8,128)(2,1)S(1)} %multiply_convert_fusion.1), kind=kOutput, calls=%fused_computation.14 | convolution fusion | flops 44040192 | bytes 12675072 | tf_op jit(solution)/shard_map/tbc,tdc->tbd/dot_general | solution.py:361
  59.1 0.0 copy-done.2
  59.1 2.4 copy.29
  61.5 207.4 %grads_rs.1 = (f32[8,128]{1,0:T(8,128)}, f32[64,128]{1,0:T(8,128)}, f32[64,128]{1,0:T(8,128)}) custom-call(f32[8,128]{1,0:T(8,128)} %broadcast_in_dim.2.cnt_ref, bf16[4,512,2048]{2,1,0:T(8,128)(2,1)} %bitcast.27, bf16[512,2048]{1,0:T(8,128)(2,1)} %bitcast.28, bf16[6,2048,512]{2,1,0:T(8,128)(2,1)} %convolution_convert_fusion.dz_hbm, ...), custom_call_target="tpu_custom_call" | custom-call | tf_op jit(solution)/shard_map/grads_rs/pallas_call | solution.py:331
  268.9 1.2 slice_bitcast_fusion
  270.1 1.4 copy.42
  271.5 1.4 copy.43
  (3 shorter events, 0.1 us)
Async XLA Ops:
  0.6 44.0 %copy-start = (bf16[6,512,3]{1,2,0:T(4,128)(2,1)S(1)}, bf16[6,512,3]{1,2,0:T(4,128)(2,1)}, u32[]{:S(2)}) copy-start(bf16[6,512,3]{1,2,0:T(4,128)(2,1)} %param.9) | copy-start | bytes 55300
  33.7 8.4 %copy-start.1 = (bf16[2048,512]{1,0:T(8,128)(2,1)S(1)}, bf16[2048,512]{1,0:T(8,128)(2,1)}, u32[]{:S(2)}) copy-start(bf16[2048,512]{1,0:T(8,128)(2,1)} %param.6) | copy-start | bytes 6291460
  44.6 8.1 %copy-start.3 = (s32[6,2048]{1,0:T(8,128)S(1)}, s32[6,2048]{1,0:T(8,128)}, u32[]{:S(2)}) copy-start(s32[6,2048]{1,0:T(8,128)} %param.10) | copy-start | bytes 147460
  52.6 6.5 %copy-start.2 = (bf16[2048,512]{1,0:T(8,128)(2,1)S(1)}, bf16[2048,512]{1,0:T(8,128)(2,1)}, u32[]{:S(2)}) copy-start(bf16[2048,512]{1,0:T(8,128)(2,1)} %param.8) | copy-start | bytes 6291460

commit v2 on v1

--- a/solution.py
+++ b/solution.py
@@ -56,26 +56,32 @@
         c.start()
 
     barrier = pltpu.get_barrier_semaphore()
-    peers = [(partner,)] + [nb(d, s) for d in range(3) for s in (1, -1)]
+    peers = [(partner,)] + [nb(d, s) for d in range(3) for s in (1, -1, 2)]
     for p in peers:
         pl.semaphore_signal(barrier, inc=1, device_id=p, device_id_type=MESH)
-    pl.semaphore_wait(barrier, 7)
+    pl.semaphore_wait(barrier, 10)
 
     def all_reduce(base, val):
-        plist = [(partner,)]
-        for d in range(3):
-            odd = lax.rem(coord[d], 2)
-            plist.append(nb(d, 1 - 2 * odd))
-            plist.append(nb(d, 2 * odd - 1))
-        for i, p in enumerate(plist):
-            s = base + i
+        ar_s[base] = val
+        cp = pltpu.make_async_remote_copy(
+            src_ref=ar_s.at[base], dst_ref=ar_r.at[base, 0], send_sem=ars_sem.at[base], recv_sem=arr_sem.at[base],
+            device_id=(partner,), device_id_type=MESH)
+        cp.start()
+        cp.wait()
+        val = val + ar_r[base, 0]
+        for dim in range(3):
+            s = base + 1 + dim
+            u = coord[dim]
             ar_s[s] = val
-            cp = pltpu.make_async_remote_copy(
-                src_ref=ar_s.at[s], dst_ref=ar_r.at[s], send_sem=ars_sem.at[s], recv_sem=arr_sem.at[s],
-                device_id=p, device_id_type=MESH)
-            cp.start()
-            cp.wait()
-            val = val + ar_r[s]
+            for step in (2, 1, 3):
+                pltpu.make_async_remote_copy(
+                    src_ref=ar_s.at[s], dst_ref=ar_r.at[s, u], send_sem=ars_sem.at[s], recv_sem=arr_sem.at[s],
+                    device_id=nb(dim, step), device_id_type=MESH).start()
+            three = ar_r.at[s, pl.ds(0, 3)]
+            pltpu.make_async_copy(three, three, arr_sem.at[s]).wait()
+            pltpu.make_async_copy(three, three, ars_sem.at[s]).wait()
+            part = [jnp.where(u == i, val, ar_r[s, i]) for i in range(4)]
+            val = (part[0] + part[1]) + (part[2] + part[3])
         return val
 
     total = all_reduce(0, cnt_ref[...])
@@ -184,11 +190,9 @@
             for t in range(3):
                 dz_loads[3 * half + t].wait()
 
-        def task(t, _):
+        for t in range(3 * half, 3 * half + 3):
             acc = jnp.dot(aT[rb], dz[t, :, cols], preferred_element_type=F32)
             emit(hs, t, acc)
-            return 0
-        lax.fori_loop(3 * half, 3 * half + 3, task, 0)
 
     def compute_in(k, half):
         fb = lax.div(k, 2)
@@ -203,20 +207,12 @@
             @pl.when(fb + 1 < nfb)
             def _():
                 gp_load(fb + 1).start()
-        tok = q.shape[0]
-        step = tok // 4
-
-        def task(t, _):
-            def tile(i, _):
-                rows = pl.ds(pl.multiple_of(i * step, step), step)
-                d_act = jnp.dot(dz[t, rows, :], w2T[fb], preferred_element_type=F32)
-                q[rows, :] = (d_act * gp[gs, rows, :]).astype(BF16)
-                return 0
-            lax.fori_loop(0, 4, tile, 0)
-            acc = jnp.dot(xT[...], q[...], preferred_element_type=F32)
+
+        for t in range(3 * half, 3 * half + 3):
+            d_act = jnp.dot(dz[t], w2T[fb], preferred_element_type=F32)
+            q[t % 2] = (d_act * gp[gs]).astype(BF16)
+            acc = jnp.dot(xT[...], q[t % 2], preferred_element_type=F32)
             emit(hs, t, acc)
-            return 0
-        lax.fori_loop(3 * half, 3 * half + 3, task, 0)
 
     def compute(k, half):
         @pl.when(k < nchunk)
@@ -274,7 +270,7 @@
         val = jnp.sum(jnp.sum(acc, axis=0, keepdims=True), axis=1, keepdims=True)
         hit = ((row_id == t) & (col_id == s)) | ((row_id == s) & (col_id == t))
         gram = jnp.where(hit, val, gram)
-    gram = all_reduce(7, gram)
+    gram = all_reduce(4, gram)
 
     diag = jnp.where(row_id == col_id, gram, 0.0)
     scale = jnp.sum(jnp.sum(diag, axis=0, keepdims=True), axis=1, keepdims=True) / T
@@ -336,13 +332,13 @@
         out_specs=[vm] * 3,
         scratch_shapes=[
             V((rb, 512, tok), BF16), V((512, tok), BF16), V((T, tok, 512), BF16), V((2 * rb, 512, 256), BF16),
-            V((2, tok, 256), F32), V((tok, 256), BF16), V((T, 8, 128), F32),
+            V((2, tok, 256), F32), V((2, tok, 256), BF16), V((T, 8, 128), F32),
             V((2, 2, T, 512, 128), BF16), V((XRING, T, 512, 128), BF16),
             V((DEPTH, T, 4, 4, 4, 8, 128), F32), V((DEPTH, T, 4, 4, 8, 128), F32), V((DEPTH, T, 4, 8, 128), F32),
             V((RING, 3, T, 4, 4, 8, 128), F32), V((RING, 3, T, 4, 8, 128), F32), V((RING, 3, T, 8, 128), F32),
-            V((T, nchunk, 8, 128), F32), V((2, nchunk, 8, 128), F32), V((14, 8, 128), F32), V((14, 8, 128), F32),
+            V((T, nchunk, 8, 128), F32), V((2, nchunk, 8, 128), F32), V((8, 8, 128), F32), V((8, 4, 8, 128), F32),
             DS((rb + T + 2,)), DS((2,)), DS((2, 2)), DS((XRING, 2)), DS((3, DEPTH)), DS((3, 2, RING)),
-            DS((14,)), DS((14,)), DS, DS,
+            DS((8,)), DS((8,)), DS, DS,
         ],
         compiler_params=pltpu.CompilerParams(collective_id=0, has_side_effects=True, vmem_limit_bytes=66 * 1000 * 1000),
     )(cnt, aT, xT, dz, w2T, gp)

time: 274 us -> 232 us (0.85)
  Pallas kernels: 207 us -> 166 us
    pallas_call x1, Pallas kernels: 207 us -> 166 us  [reduce_and_solve(): pl.pallas_call(functools.partial(kernel, rb), name='grads_rs', out_shape=...]
where the time goes in v2:
time: 232 us; the launch traced here: 231 us
  Pallas kernels  166 us (72%)
  matrix products  33.4 us (14%)
  local copies, waits for them, and re-layouts  30.2 us (13%)
    pallas_call x1, Pallas kernels, reduce_and_solve(): pl.pallas_call(functools.partial(kernel, rb), name='grads_rs', out_shape=...  166 us
    dot_general x1, matrix products, forward(): pre_act = jnp.dot(x_loc, w_in, preferred_element_type=F32)  19 us
    convert_element_type x1, local copies, waits for them, and re-layouts, forward(): act_bf = act_out.astype(BF16)  12.3 us
    transpose x1, local copies, waits for them, and re-layouts, local_step(): aT = act.reshape(tok, 64, rb, 8).transpose(2, 1, 3, 0).reshape(rb, 512, tok)  8.41 us
    dot_general x1, matrix products, forward(): jnp.einsum('bd,tdc->tbc', z_bf, task_heads, preferred_element_type=F32)  7.99 us
    dot_general x1, matrix products, forward(): jnp.einsum('tbc,tdc->tbd', d_logit, task_heads, preferred_element_type=F32)  6.38 us
    unnamed x11, local copies, waits for them, and re-layouts  5.22 us

profile of v2, /device:TPU:1, one launch (start us, length us, event | category | flops | bytes accessed | tf_op | source)
XLA Modules:
  0.0 231.4 jit_solution(1857275110356331650)
XLA Ops:
  0.6 0.0 copy-start
  0.6 1.0 fusion.14
  1.7 0.7 broadcast_in_dim.2.cnt_ref
  2.4 19.0 %fusion.9 = (f32[2048,2048]{1,0:T(8,128)}, bf16[2048,2048]{1,0:T(8,128)(2,1)}) fusion(bf16[2048,512]{1,0:T(8,128)(2,1)} %param.6, bf16[512,2048]{1,0:T(8,128)(2,1)} %param.7), kind=kOutput, calls=%fused_computation.11 | convolution fusion | flops 4370464768 | bytes 29360128 | tf_op jit(solution)/shard_map/dot_general | solution.py:348
  21.4 12.3 %copy.24 = bf16[2048,2048]{0,1:T(8,128)(2,1)} copy(bf16[2048,2048]{1,0:T(8,128)(2,1)} %get-tuple-element.10) | data formatting | bytes 16777216 | tf_op jit(solution)/shard_map/convert_element_type | solution.py:350
  33.7 0.0 copy-start.1
  33.7 8.4 %copy.39 = bf16[4,64,8,2048]{3,2,1,0:T(8,128)(2,1)} copy(bf16[4,64,8,2048]{3,2,0,1:T(8,128)(2,1)} %bitcast.26) | data formatting | bytes 16777216 | tf_op jit(solution)/shard_map/transpose | solution.py:369
  42.1 0.0 copy-done.1
  42.1 2.4 %copy.26 = bf16[2048,512]{0,1:T(8,128)(2,1)} copy(bf16[2048,512]{1,0:T(8,128)(2,1)S(1)} %copy-done.1) | data formatting | bytes 4194304 | tf_op args[0]
  44.6 0.0 copy-done
  44.6 0.0 copy-start.3
  44.6 8.0 %fusion.15 = (f32[6,2048]{1,0:T(8,128)S(1)}, f32[6,2048,3]{1,0,2:T(8,128)S(1)}) fusion(bf16[6,512,3]{1,2,0:T(4,128)(2,1)S(1)} %copy-done, bf16[2048,2048]{1,0:T(8,128)(2,1)} %get-tuple-element.10, bf16[2048,512]{1,0:T(8,128)(2,1)} %param.8, bf16[2048,512]{1,0:T(8,128)(2,1)S(1)} %copy-done.1), kind=kOutput, calls=%fused_computation.26 | convolution fusion | flops 4335886336 | bytes 12797952 | tf_op jit(solution)/shard_map/bd,tdc->tbc/dot_general | solution.py:353
  52.6 0.0 copy-start.2
  52.7 0.0 copy-done.3
  52.7 0.1 multiply_convert_fusion.1
  52.7 6.4 %convolution_convert_fusion.dz_hbm = bf16[6,2048,512]{2,1,0:T(8,128)(2,1)} fusion(bf16[6,512,3]{1,2,0:T(4,128)(2,1)S(1)} %copy-done, bf16[6,2048,3]{1,0,2:T(8,128)(2,1)S(1)} %multiply_convert_fusion.1), kind=kOutput, calls=%fused_computation.14 | convolution fusion | flops 44040192 | bytes 12675072 | tf_op jit(solution)/shard_map/tbc,tdc->tbd/dot_general | solution.py:357
  59.1 0.0 copy-done.2
  59.1 2.4 %copy.29 = bf16[8,256,512]{1,2,0:T(8,128)(2,1)} copy(bf16[8,256,512]{2,1,0:T(8,128)(2,1)S(1)} %bitcast.30) | data formatting | bytes 4194304 | tf_op jit(solution)/shard_map/reshape | solution.py:370
  61.5 165.9 %grads_rs.1 = (f32[8,128]{1,0:T(8,128)}, f32[64,128]{1,0:T(8,128)}, f32[64,128]{1,0:T(8,128)}) custom-call(f32[8,128]{1,0:T(8,128)} %broadcast_in_dim.2.cnt_ref, bf16[4,512,2048]{2,1,0:T(8,128)(2,1)} %bitcast.27, bf16[512,2048]{1,0:T(8,128)(2,1)} %bitcast.28, bf16[6,2048,512]{2,1,0:T(8,128)(2,1)} %convolution_convert_fusion.dz_hbm, ...), custom_call_target="tpu_custom_call" | custom-call | tf_op jit(solution)/shard_map/grads_rs/pallas_call | solution.py:327
  227.5 1.2 slice_bitcast_fusion
  228.7 1.4 copy.42
  230.0 1.4 copy.43
  (3 shorter events, 0.1 us)
Async XLA Ops:
  0.6 44.0 %copy-start = (bf16[6,512,3]{1,2,0:T(4,128)(2,1)S(1)}, bf16[6,512,3]{1,2,0:T(4,128)(2,1)}, u32[]{:S(2)}) copy-start(bf16[6,512,3]{1,2,0:T(4,128)(2,1)} %param.9) | copy-start | bytes 55300
  33.7 8.4 %copy-start.1 = (bf16[2048,512]{1,0:T(8,128)(2,1)S(1)}, bf16[2048,512]{1,0:T(8,128)(2,1)}, u32[]{:S(2)}) copy-start(bf16[2048,512]{1,0:T(8,128)(2,1)} %param.6) | copy-start | bytes 6291460
  44.6 8.1 %copy-start.3 = (s32[6,2048]{1,0:T(8,128)S(1)}, s32[6,2048]{1,0:T(8,128)}, u32[]{:S(2)}) copy-start(s32[6,2048]{1,0:T(8,128)} %param.10) | copy-start | bytes 147460
  52.6 6.5 %copy-start.2 = (bf16[2048,512]{1,0:T(8,128)(2,1)S(1)}, bf16[2048,512]{1,0:T(8,128)(2,1)}, u32[]{:S(2)}) copy-start(bf16[2048,512]{1,0:T(8,128)(2,1)} %param.8) | copy-start | bytes 6291460

commit v3 on v2

--- a/solution.py
+++ b/solution.py
@@ -19,12 +19,11 @@
     return ((z, y, x), (y, x, z), (x, z, y))[order]
 
 
-def kernel(rb_count, cnt_ref, aT_hbm, xT_hbm, dz_hbm, w2T_hbm, gp_hbm,
-           alpha_ref, out1_ref, out2_ref,
-           aT, xT, dz, w2T, gp, q, inv, hb, xr, dbuf, ebuf, fbuf, r1, r2, r3, shard, gb, ar_s, ar_r,
+def kernel(code_ref, ht3_ref, ht24_ref, x_hbm, w1_hbm, w2_hbm,
+           alpha_ref, out1_ref, out2_ref, gp_hbm,
+           aT, xT, dz, w2, gp, q, hbig, inv, hb, xr, dbuf, ebuf, fbuf, r1, r2, r3, shard, gb, ar_s, ar_r,
            ld_sem, gp_sem, xs_sem, xr_sem, s_sem, r_sem, ars_sem, arr_sem, gs_sem, gr_sem):
-    nchunk = 4 * rb_count
-    nfb = 2 * rb_count
+    nchunk, nfb = 16, 8
     me = lax.axis_index("data")
     core = lax.rem(me, 2)
     coord = (lax.div(me, 32), lax.rem(lax.div(me, 8), 4), lax.rem(lax.div(me, 2), 4))
@@ -37,23 +36,17 @@
     def rel(dim, step):
         return lax.rem(coord[dim] + step + 4, 4)
 
-    loads = [pltpu.make_async_copy(aT_hbm.at[i], aT.at[i], ld_sem.at[i]) for i in range(rb_count)]
-    dz_loads = [pltpu.make_async_copy(dz_hbm.at[t], dz.at[t], ld_sem.at[rb_count + t]) for t in range(T)]
-    x_load = pltpu.make_async_copy(xT_hbm, xT, ld_sem.at[rb_count + T])
-    w_load = pltpu.make_async_copy(w2T_hbm, w2T, ld_sem.at[rb_count + T + 1])
+    x_loads = [pltpu.make_async_copy(x_hbm.at[:, pl.ds(256 * i, 256)], q.at[i], ld_sem.at[i]) for i in range(2)]
+    w1_load = pltpu.make_async_copy(w1_hbm, xT, ld_sem.at[2])
+    w2_load = pltpu.make_async_copy(w2_hbm, w2, ld_sem.at[3])
+    for c in x_loads + [w1_load, w2_load]:
+        c.start()
 
     def gp_load(fb):
-        cols = pl.ds(pl.multiple_of(fb * 256, 256), 256)
-        return pltpu.make_async_copy(gp_hbm.at[:, cols], gp.at[lax.rem(fb, 2)], gp_sem.at[lax.rem(fb, 2)])
-
-    loads[0].start()
-    for c in dz_loads:
-        c.start()
-    w_load.start()
-    x_load.start()
-    gp_load(0).start()
-    for c in loads[1:]:
-        c.start()
+        return pltpu.make_async_copy(gp_hbm.at[fb], gp.at[lax.rem(fb, 2)], gp_sem.at[lax.rem(fb, 2)])
+
+    def gp_store(fb):
+        return pltpu.make_async_copy(gp.at[lax.rem(fb, 2)], gp_hbm.at[fb], gp_sem.at[lax.rem(fb, 2)])
 
     barrier = pltpu.get_barrier_semaphore()
     peers = [(partner,)] + [nb(d, s) for d in range(3) for s in (1, -1, 2)]
@@ -61,33 +54,107 @@
         pl.semaphore_signal(barrier, inc=1, device_id=p, device_id_type=MESH)
     pl.semaphore_wait(barrier, 10)
 
-    def all_reduce(base, val):
-        ar_s[base] = val
-        cp = pltpu.make_async_remote_copy(
+    def ar_core(base):
+        return pltpu.make_async_remote_copy(
             src_ref=ar_s.at[base], dst_ref=ar_r.at[base, 0], send_sem=ars_sem.at[base], recv_sem=arr_sem.at[base],
             device_id=(partner,), device_id_type=MESH)
-        cp.start()
-        cp.wait()
-        val = val + ar_r[base, 0]
-        for dim in range(3):
-            s = base + 1 + dim
-            u = coord[dim]
-            ar_s[s] = val
-            for step in (2, 1, 3):
-                pltpu.make_async_remote_copy(
-                    src_ref=ar_s.at[s], dst_ref=ar_r.at[s, u], send_sem=ars_sem.at[s], recv_sem=arr_sem.at[s],
-                    device_id=nb(dim, step), device_id_type=MESH).start()
-            three = ar_r.at[s, pl.ds(0, 3)]
-            pltpu.make_async_copy(three, three, arr_sem.at[s]).wait()
-            pltpu.make_async_copy(three, three, ars_sem.at[s]).wait()
-            part = [jnp.where(u == i, val, ar_r[s, i]) for i in range(4)]
-            val = (part[0] + part[1]) + (part[2] + part[3])
+
+    def ar_start(base, stage, val):
+        s = base + stage
+        ar_s[s] = val
+        if stage == 0:
+            ar_core(base).start()
+            return
+        dim = stage - 1
+        for step in (2, 1, 3):
+            pltpu.make_async_remote_copy(
+                src_ref=ar_s.at[s], dst_ref=ar_r.at[s, coord[dim]], send_sem=ars_sem.at[s], recv_sem=arr_sem.at[s],
+                device_id=nb(dim, step), device_id_type=MESH).start()
+
+    def ar_finish(base, stage):
+        s = base + stage
+        if stage == 0:
+            ar_core(base).wait()
+            return ar_s[s] + ar_r[s, 0]
+        three = ar_r.at[s, pl.ds(0, 3)]
+        pltpu.make_async_copy(three, three, arr_sem.at[s]).wait()
+        pltpu.make_async_copy(three, three, ars_sem.at[s]).wait()
+        u = coord[stage - 1]
+        part = [jnp.where(u == i, ar_s[s], ar_r[s, i]) for i in range(4)]
+        return (part[0] + part[1]) + (part[2] + part[3])
+
+    def all_reduce(base, val):
+        for stage in range(4):
+            ar_start(base, stage, val)
+            val = ar_finish(base, stage)
         return val
 
-    total = all_reduce(0, cnt_ref[...])
-    inv_all = 1.0 / jnp.maximum(total, 1.0)
+    cnt = jnp.sum((code_ref[0:8, :] >= 0).astype(F32), axis=1, keepdims=True)
+    ar_start(0, 0, jnp.broadcast_to(cnt, (8, 128)))
+    for c in x_loads + [w1_load]:
+        c.wait()
+    K0, K1 = 0.7978845608028654, 0.044715
+
+    def hidden(fb, _):
+        cols = pl.ds(pl.multiple_of(fb * 256, 256), 256)
+        for stage in range(1, 4):
+            @pl.when(fb == 2 * stage)
+            def _():
+                ar_start(0, stage, ar_finish(0, stage - 1))
+
+        @pl.when(fb >= 2)
+        def _():
+            gp_store(fb - 2).wait()
+        for i in range(4):
+            rows = slice(512 * i, 512 * i + 512)
+            p = (jnp.dot(q[0, rows, :], xT[0:256, cols], preferred_element_type=F32)
+                 + jnp.dot(q[1, rows, :], xT[256:512, cols], preferred_element_type=F32))
+            p2 = p * p
+            th = jnp.tanh(p * (K0 + (K0 * K1) * p2))
+            cdf = 0.5 + 0.5 * th
+            act = (p * cdf).astype(BF16)
+            gp[lax.rem(fb, 2), rows, :] = cdf + (0.5 - 0.5 * (th * th)) * (p * (K0 + (3 * K0 * K1) * p2))
+            dz[lax.div(fb, 2), rows, pl.ds(pl.multiple_of(lax.rem(fb, 2) * 256, 256), 256)] = act
+            aT[pl.ds(fb * 8, 8), :, :, rows] = act.T.reshape(8, 2, 16, 512)
+        gp_store(fb).start()
+        return 0
+    lax.fori_loop(0, nfb, hidden, 0)
+    gp_store(nfb - 2).wait()
+    gp_store(nfb - 1).wait()
+    gp_load(0).start()
+
+    inv_all = 1.0 / jnp.maximum(ar_finish(0, 3), 1.0)
     for t in range(T):
         inv[t] = jnp.broadcast_to(inv_all[t:t + 1, :], (8, 128))
+
+    head_row = lax.rem(lax.broadcasted_iota(jnp.int32, (128, 512), 0), 8)
+    for t in range(T):
+        hbig[t] = jnp.where(head_row == t, ht24_ref[...].astype(F32), 0.0).astype(BF16)
+    w2_load.wait()
+
+    def tokens(i, _):
+        rows = pl.ds(pl.multiple_of(i * 512, 512), 512)
+        z = jnp.dot(dz[0, rows, :], w2[0:512, :], preferred_element_type=F32)
+        for j in range(1, 4):
+            z = z + jnp.dot(dz[j, rows, :], w2[512 * j:512 * j + 512, :], preferred_element_type=F32)
+        x_t = jnp.concatenate([q[0, rows, :], q[1, rows, :]], axis=1)
+        zb = (x_t.astype(F32) + z).astype(BF16)
+        logits = lax.dot_general(zb, ht3_ref[...], (((1,), (1,)), ((), ())), preferred_element_type=F32)
+        ls = [logits[:, 128 * c:128 * c + 128] for c in range(3)]
+        top = jnp.maximum(jnp.maximum(ls[0], ls[1]), ls[2])
+        ex = [jnp.exp(v - top) for v in ls]
+        den = ex[0] + ex[1] + ex[2]
+        code = code_ref[:, rows].T
+        errs = []
+        for c in range(3):
+            err = jnp.where(code >= 0, ex[c] / den - (code == c).astype(F32), 0.0)
+            errs.append(err.astype(BF16).astype(F32))
+        packed = (errs[0] + pltpu.roll(errs[1], 8, 1) + pltpu.roll(errs[2], 16, 1)).astype(BF16)
+        for t in range(T):
+            dz[t, rows, :] = jnp.dot(packed, hbig[t], preferred_element_type=F32).astype(BF16)
+        xT[:, rows] = x_t.T
+        return 0
+    lax.fori_loop(0, 4, tokens, 0)
 
     srcs = (dbuf, ebuf, fbuf)
     recvs = (r1, r2, r3)
@@ -147,7 +214,7 @@
     def half_copy(k, half):
         hs, xs = lax.rem(k, 2), lax.rem(k, XRING)
         return pltpu.make_async_remote_copy(
-            src_ref=hb.at[hs, 1 - core, pl.ds(3 * half, 3)], dst_ref=xr.at[xs, pl.ds(3 * half, 3)],
+            src_ref=hb.at[hs, 1 - core, pl.ds(4 * half, 4 - 2 * half)], dst_ref=xr.at[xs, pl.ds(4 * half, 4 - 2 * half)],
             send_sem=xs_sem.at[hs, half], recv_sem=xr_sem.at[xs, half],
             device_id=(partner,), device_id_type=MESH)
 
@@ -169,50 +236,37 @@
                     dbuf[d, t, a, b, c] = s[8 * e:8 * e + 8]
         open_phase(0, k)
 
-    def emit(hs, t, acc):
-        row = inv[t][0:1, :]
-        hb[hs, 0, t] = (acc[:, :128] * row).astype(BF16)
-        hb[hs, 1, t] = (acc[:, 128:] * row).astype(BF16)
-
     def compute_out(k, half):
         j = lax.div(k, 2)
-        rb, cb = lax.div(j, 2), lax.rem(j, 2)
+        h, cb = lax.div(j, 4), lax.rem(j, 4)
         hs = lax.rem(k, 2)
-        cols = pl.ds(pl.multiple_of(cb * 256, 256), 256)
-        if half == 0:
-            for i in range(rb_count):
-                @pl.when(j == 2 * i)
-                def _():
-                    loads[i].wait()
-
-        @pl.when(k == 0)
-        def _():
-            for t in range(3):
-                dz_loads[3 * half + t].wait()
-
-        for t in range(3 * half, 3 * half + 3):
-            acc = jnp.dot(aT[rb], dz[t, :, cols], preferred_element_type=F32)
-            emit(hs, t, acc)
+        cols = pl.ds(pl.multiple_of(cb * 128, 128), 128)
+        lhs = aT[:, h, :, :].reshape(1024, 2048)
+        for t in ((0, 2), (4,))[half]:
+            rhs = jnp.concatenate([dz[t, :, cols], dz[t + 1, :, cols]], axis=1)
+            acc = jnp.dot(lhs, rhs, preferred_element_type=F32)
+            for e in range(2):
+                part = (acc[:, 128 * e:128 * e + 128] * inv[t + e][0:1, :]).reshape(64, 2, 8, 128)
+                for c in range(2):
+                    hb[hs, c, t + e] = part[:, c].reshape(512, 128).astype(BF16)
 
     def compute_in(k, half):
         fb = lax.div(k, 2)
         hs, gs = lax.rem(k, 2), lax.rem(fb, 2)
         if half == 0:
-            @pl.when(k == 1)
-            def _():
-                w_load.wait()
-                x_load.wait()
             gp_load(fb).wait()
 
             @pl.when(fb + 1 < nfb)
             def _():
                 gp_load(fb + 1).start()
-
-        for t in range(3 * half, 3 * half + 3):
-            d_act = jnp.dot(dz[t], w2T[fb], preferred_element_type=F32)
+        w_blk = w2[pl.ds(pl.multiple_of(fb * 256, 256), 256), :]
+        for t in range(4 * half, 4 + 2 * half):
+            d_act = lax.dot_general(dz[t], w_blk, (((1,), (1,)), ((), ())), preferred_element_type=F32)
             q[t % 2] = (d_act * gp[gs]).astype(BF16)
             acc = jnp.dot(xT[...], q[t % 2], preferred_element_type=F32)
-            emit(hs, t, acc)
+            row = inv[t][0:1, :]
+            hb[hs, 0, t] = (acc[:, :128] * row).astype(BF16)
+            hb[hs, 1, t] = (acc[:, 128:] * row).astype(BF16)
 
     def compute(k, half):
         @pl.when(k < nchunk)
@@ -308,67 +362,48 @@
             for r in range(4):
                 o = r * 2 * nfb + 2 * fb + h
                 out1_ref[o:o + 1, :] = rows[r:r + 1]
-        for rbl in range(rb_count // 2):
-            for cb in range(2):
-                tile = gb[h, 4 * ((rb_count // 2) * core + rbl) + 2 * cb]
-                for r in range(8):
-                    o = (8 * rbl + r) * 4 + 2 * cb + h
-                    out2_ref[o:o + 1, :] = tile[r:r + 1]
-
-
-def reduce_and_solve(cnt, aT, xT, dz, w2T, gp):
-    rb, _, tok = aT.shape
-    nchunk = 4 * rb
+        for cb in range(4):
+            tile = gb[h, 2 * (4 * core + cb)]
+            for r in range(8):
+                o = (8 * h + r) * 4 + cb
+                out2_ref[o:o + 1, :] = tile[r:r + 1]
+
+
+def reduce_and_solve(code, ht3, ht24, x_loc, w_in, w_out):
     any_spec = pl.BlockSpec(memory_space=pl.ANY)
     vm = pl.BlockSpec(memory_space=pltpu.VMEM)
-    rows = 4 * rb * 512 // 128
     V = pltpu.VMEM
     DS = pltpu.SemaphoreType.DMA
+    shapes = [(8, 128), (64, 128), (64, 128), (8, 2048, 256)]
     return pl.pallas_call(
-        functools.partial(kernel, rb),
+        kernel,
         name="grads_rs",
-        out_shape=[jax.ShapeDtypeStruct((8, 128), F32), jax.ShapeDtypeStruct((rows, 128), F32), jax.ShapeDtypeStruct((rows, 128), F32)],
-        in_specs=[vm] + [any_spec] * 5,
-        out_specs=[vm] * 3,
+        out_shape=[jax.ShapeDtypeStruct(s, F32) for s in shapes],
+        in_specs=[vm] * 3 + [any_spec] * 3,
+        out_specs=[vm] * 3 + [any_spec],
         scratch_shapes=[
-            V((rb, 512, tok), BF16), V((512, tok), BF16), V((T, tok, 512), BF16), V((2 * rb, 512, 256), BF16),
-            V((2, tok, 256), F32), V((2, tok, 256), BF16), V((T, 8, 128), F32),
+            V((64, 2, 16, 2048), BF16), V((512, 2048), BF16), V((T, 2048, 512), BF16), V((2048, 512), BF16),
+            V((2, 2048, 256), F32), V((2, 2048, 256), BF16), V((T, 128, 512), BF16), V((T, 8, 128), F32),
             V((2, 2, T, 512, 128), BF16), V((XRING, T, 512, 128), BF16),
             V((DEPTH, T, 4, 4, 4, 8, 128), F32), V((DEPTH, T, 4, 4, 8, 128), F32), V((DEPTH, T, 4, 8, 128), F32),
             V((RING, 3, T, 4, 4, 8, 128), F32), V((RING, 3, T, 4, 8, 128), F32), V((RING, 3, T, 8, 128), F32),
-            V((T, nchunk, 8, 128), F32), V((2, nchunk, 8, 128), F32), V((8, 8, 128), F32), V((8, 4, 8, 128), F32),
-            DS((rb + T + 2,)), DS((2,)), DS((2, 2)), DS((XRING, 2)), DS((3, DEPTH)), DS((3, 2, RING)),
+            V((T, 16, 8, 128), F32), V((2, 16, 8, 128), F32), V((8, 8, 128), F32), V((8, 4, 8, 128), F32),
+            DS((4,)), DS((2,)), DS((2, 2)), DS((XRING, 2)), DS((3, DEPTH)), DS((3, 2, RING)),
             DS((8,)), DS((8,)), DS, DS,
         ],
-        compiler_params=pltpu.CompilerParams(collective_id=0, has_side_effects=True, vmem_limit_bytes=66 * 1000 * 1000),
-    )(cnt, aT, xT, dz, w2T, gp)
-
-
-def forward(x_loc, w_in, w_out, task_heads, lab_loc, mask_loc):
-    pre_act = jnp.dot(x_loc, w_in, preferred_element_type=F32)
-    act_out, gelu_slope = jax.jvp(jax.nn.gelu, (pre_act,), (jnp.ones_like(pre_act),))
-    act_bf = act_out.astype(BF16)
-    residual = x_loc.astype(F32) + jnp.dot(act_bf, w_out, preferred_element_type=F32)
-    z_bf = residual.astype(BF16)
-    logits = jnp.einsum("bd,tdc->tbc", z_bf, task_heads, preferred_element_type=F32)
-    soft_prob = jax.nn.softmax(logits, axis=-1)
-    onehot = (lab_loc[:, :, None] == jnp.arange(logits.shape[-1])).astype(F32)
-    d_logit = (mask_loc[:, :, None].astype(F32) * (soft_prob - onehot)).astype(BF16)
-    d_resid = jnp.einsum("tbc,tdc->tbd", d_logit, task_heads, preferred_element_type=F32).astype(BF16)
-    return act_bf, gelu_slope, d_resid
+        compiler_params=pltpu.CompilerParams(collective_id=0, has_side_effects=True, vmem_limit_bytes=67043328),
+    )(code, ht3, ht24, x_loc, w_in, w_out)
 
 
 def solution(mesh):
     def local_step(x_loc, w_in, w_out, task_heads, lab_loc, mask_loc):
-        tok = x_loc.shape[0]
-        hid = w_in.shape[1]
-        rb = hid // 512
-        cnt = mask_loc.sum(axis=1).astype(F32)
-        cnt = jnp.broadcast_to(jnp.pad(cnt, (0, 2))[:, None], (8, 128))
-        act, slope, dz = forward(x_loc, w_in, w_out, task_heads, lab_loc, mask_loc)
-        aT = act.reshape(tok, 64, rb, 8).transpose(2, 1, 3, 0).reshape(rb, 512, tok)
-        w2T = w_out.reshape(2 * rb, 256, 512).transpose(0, 2, 1)
-        alpha, g_in, g_out = reduce_and_solve(cnt, aT, x_loc.T, dz, w2T, slope)
+        code = jnp.where(mask_loc > 0, lab_loc, -1).astype(F32)
+        code = jnp.pad(code, ((0, 122), (0, 0)), constant_values=-1.0)
+        by_class = task_heads.transpose(2, 0, 1)
+        ht3 = jnp.pad(by_class, ((0, 0), (0, 122), (0, 0))).reshape(384, 512)
+        ht24 = jnp.pad(by_class, ((0, 0), (0, 2), (0, 0))).reshape(24, 512)
+        ht24 = jnp.pad(ht24, ((0, 104), (0, 0)))
+        alpha, g_in, g_out, _ = reduce_and_solve(code, ht3, ht24, x_loc, w_in, w_out)
         return alpha[0, :6], g_in.reshape(-1), g_out.reshape(-1)
 
     return jax.shard_map(local_step, mesh=mesh, in_specs=(P("data", None), P(), P(), P(), P(None, "data"), P(None, "data")), out_specs=(P(), P("data"), P("data")), check_vma=False)

time: 232 us -> 202 us (0.87)
  matrix products: 33.4 us -> 0 us
  Pallas kernels: 166 us -> 193 us
  local copies, waits for them, and re-layouts: 30.2 us -> 7.25 us
    dot_general x3 -> x0, matrix products: 33.4 us -> none  [the longest x1 19 us: forward(): pre_act = jnp.dot(x_loc, w_in, preferred_element_type=F32)]
    pallas_call x1, Pallas kernels: 166 us -> 193 us  [reduce_and_solve(): pl.pallas_call(kernel, name='grads_rs', out_shape=[jax.ShapeDtypeStruct(s...]
    convert_element_type x1 -> x0, local copies, waits for them, and re-layouts: 12.3 us -> none  [forward(): act_bf = act_out.astype(BF16)]
    transpose x1 -> x0, local copies, waits for them, and re-layouts: 8.41 us -> none  [local_step(): aT = act.reshape(tok, 64, rb, 8).transpose(2, 1, 3, 0).reshape(rb, 512, tok)]
    pad x1 -> x3, local copies, waits for them, and re-layouts: 0.01 us -> 2.56 us  [the longest x1 1.09 us: local_step(): code = jnp.pad(code, ((0, 122), (0, 0)), constant_values=-1.0)]
    reshape x1, local copies, waits for them, and re-layouts: 2.42 us -> 0.01 us  [local_step(): ht24 = jnp.pad(by_class, ((0, 0), (0, 2), (0, 0))).reshape(24, 512)]
    unnamed x11 -> x3, local copies, waits for them, and re-layouts: 5.22 us -> 3.49 us
where the time goes in v3:
time: 202 us
  Pallas kernels  193 us (96%)
  local copies, waits for them, and re-layouts  7.25 us (4%)
    pallas_call x1, Pallas kernels, reduce_and_solve(): pl.pallas_call(kernel, name='grads_rs', out_shape=[jax.ShapeDtypeStruct(s...  193 us

profile of v3, /device:TPU:1, one launch (start us, length us, event | category | flops | bytes accessed | tf_op | source)
XLA Modules:
  0.0 201.5 jit_solution(3493131954275293286)
XLA Ops:
  0.6 0.7 copy.11
  1.4 0.9 select_convert_fusion
  2.3 0.7 pad.19.ht24_ref
  3.0 0.8 pad.17.clone
  3.7 1.1 pad.16.code_ref
  4.8 192.7 %grads_rs.1 = (f32[8,128]{1,0:T(8,128)}, f32[64,128]{1,0:T(8,128)}, f32[64,128]{1,0:T(8,128)}, f32[8,2048,256]{2,1,0:T(8,128)}) custom-call(f32[128,2048]{1,0:T(8,128)} %pad.16.code_ref, bf16[384,512]{1,0:T(8,128)(2,1)} %bitcast.8, bf16[128,512]{1,0:T(8,128)(2,1)} %pad.19.ht24_ref, bf16[2048,512]{1,0:T(8,128)(2,1)} %x_hbm.1, bf16[512,2048]{1,0:T(8,128)(2,1)} %w1_hbm.1, ...), custom_call_target="tpu_custom_call" | custom-call | tf_op jit(solution)/shard_map/grads_rs/pallas_call | solution.py:378
  197.6 1.2 slice_bitcast_fusion
  198.8 1.4 copy.15
  200.2 1.4 copy.16
  (1 shorter events, 0.0 us)

commit v4 on v3

--- a/solution.py
+++ b/solution.py
@@ -19,9 +19,9 @@
     return ((z, y, x), (y, x, z), (x, z, y))[order]
 
 
-def kernel(code_ref, ht3_ref, ht24_ref, x_hbm, w1_hbm, w2_hbm,
+def kernel(lab_ref, mask_ref, ht24_ref, x_hbm, w1_hbm, w2_hbm,
            alpha_ref, out1_ref, out2_ref, gp_hbm,
-           aT, xT, dz, w2, gp, q, hbig, inv, hb, xr, dbuf, ebuf, fbuf, r1, r2, r3, shard, gb, ar_s, ar_r,
+           aT, xT, dz, w2, gp, q, hbig, code_ref, ht3_ref, other, inv, hb, xr, dbuf, ebuf, fbuf, r1, r2, r3, shard, gb, ar_s, ar_r,
            ld_sem, gp_sem, xs_sem, xr_sem, s_sem, r_sem, ars_sem, arr_sem, gs_sem, gr_sem):
     nchunk, nfb = 16, 8
     me = lax.axis_index("data")
@@ -89,6 +89,8 @@
             val = ar_finish(base, stage)
         return val
 
+    code_ref[...] = jnp.full(code_ref.shape, -1.0, F32)
+    code_ref[0:T, :] = jnp.where(mask_ref[...] > 0, lab_ref[...], -1).astype(F32)
     cnt = jnp.sum((code_ref[0:8, :] >= 0).astype(F32), axis=1, keepdims=True)
     ar_start(0, 0, jnp.broadcast_to(cnt, (8, 128)))
     for c in x_loads + [w1_load]:
@@ -116,20 +118,23 @@
             gp[lax.rem(fb, 2), rows, :] = cdf + (0.5 - 0.5 * (th * th)) * (p * (K0 + (3 * K0 * K1) * p2))
             dz[lax.div(fb, 2), rows, pl.ds(pl.multiple_of(lax.rem(fb, 2) * 256, 256), 256)] = act
             aT[pl.ds(fb * 8, 8), :, :, rows] = act.T.reshape(8, 2, 16, 512)
-        gp_store(fb).start()
+
+        @pl.when(fb < nfb - 2)
+        def _():
+            gp_store(fb).start()
         return 0
     lax.fori_loop(0, nfb, hidden, 0)
-    gp_store(nfb - 2).wait()
-    gp_store(nfb - 1).wait()
-    gp_load(0).start()
 
     inv_all = 1.0 / jnp.maximum(ar_finish(0, 3), 1.0)
     for t in range(T):
         inv[t] = jnp.broadcast_to(inv_all[t:t + 1, :], (8, 128))
 
+    heads = ht24_ref[...].astype(F32)
+    for c in range(3):
+        ht3_ref[128 * c:128 * c + 128, :] = jnp.concatenate([heads[8 * c:8 * c + 8], jnp.zeros((120, 512), F32)], axis=0).astype(BF16)
     head_row = lax.rem(lax.broadcasted_iota(jnp.int32, (128, 512), 0), 8)
     for t in range(T):
-        hbig[t] = jnp.where(head_row == t, ht24_ref[...].astype(F32), 0.0).astype(BF16)
+        hbig[t] = jnp.where(head_row == t, heads, 0.0).astype(BF16)
     w2_load.wait()
 
     def tokens(i, _):
@@ -211,17 +216,17 @@
         if p < 2:
             open_phase(p + 1, k)
 
-    def half_copy(k, half):
+    def pair_copy(k, third):
         hs, xs = lax.rem(k, 2), lax.rem(k, XRING)
         return pltpu.make_async_remote_copy(
-            src_ref=hb.at[hs, 1 - core, pl.ds(4 * half, 4 - 2 * half)], dst_ref=xr.at[xs, pl.ds(4 * half, 4 - 2 * half)],
-            send_sem=xs_sem.at[hs, half], recv_sem=xr_sem.at[xs, half],
+            src_ref=hb.at[hs, 1 - core, pl.ds(2 * third, 2)], dst_ref=xr.at[xs, pl.ds(2 * third, 2)],
+            send_sem=xs_sem.at[hs, third], recv_sem=xr_sem.at[xs, third],
             device_id=(partner,), device_id_type=MESH)
 
     def merge(k):
         d, hs, xs = lax.rem(k, DEPTH), lax.rem(k, 2), lax.rem(k, XRING)
-        half_copy(k, 0).wait_recv()
-        half_copy(k, 1).wait_recv()
+        for third in range(3):
+            pair_copy(k, third).wait_recv()
 
         @pl.when(k >= DEPTH)
         def _():
@@ -236,80 +241,86 @@
                     dbuf[d, t, a, b, c] = s[8 * e:8 * e + 8]
         open_phase(0, k)
 
-    def compute_out(k, half):
+    def compute_out(k, third):
         j = lax.div(k, 2)
         h, cb = lax.div(j, 4), lax.rem(j, 4)
-        hs = lax.rem(k, 2)
+        hs, t = lax.rem(k, 2), 2 * third
         cols = pl.ds(pl.multiple_of(cb * 128, 128), 128)
         lhs = aT[:, h, :, :].reshape(1024, 2048)
-        for t in ((0, 2), (4,))[half]:
-            rhs = jnp.concatenate([dz[t, :, cols], dz[t + 1, :, cols]], axis=1)
-            acc = jnp.dot(lhs, rhs, preferred_element_type=F32)
-            for e in range(2):
-                part = (acc[:, 128 * e:128 * e + 128] * inv[t + e][0:1, :]).reshape(64, 2, 8, 128)
-                for c in range(2):
-                    hb[hs, c, t + e] = part[:, c].reshape(512, 128).astype(BF16)
-
-    def compute_in(k, half):
-        fb = lax.div(k, 2)
-        hs, gs = lax.rem(k, 2), lax.rem(fb, 2)
-        if half == 0:
+        rhs = jnp.concatenate([dz[t, :, cols], dz[t + 1, :, cols]], axis=1)
+        acc = jnp.dot(lhs, rhs, preferred_element_type=F32)
+        for e in range(2):
+            part = (acc[:, 128 * e:128 * e + 128] * inv[t + e][0:1, :]).reshape(64, 2, 8, 128)
+            for c in range(2):
+                hb[hs, c, t + e] = part[:, c].reshape(512, 128).astype(BF16)
+
+    def compute_in(k, third):
+        fb = lax.rem(lax.div(k, 2) + nfb - 2, nfb)
+        hs, gs, t = lax.rem(k, 2), lax.rem(fb, 2), 2 * third
+
+        @pl.when((third == 0) & (fb < nfb - 2))
+        def _():
             gp_load(fb).wait()
 
-            @pl.when(fb + 1 < nfb)
+        @pl.when((third == 0) & (fb != nfb - 2) & (fb != nfb - 3))
+        def _():
+            gp_load(lax.rem(fb + 1, nfb)).start()
+        w_blk = w2[pl.ds(pl.multiple_of(fb * 256, 256), 256), :]
+        for e in range(2):
+            d_act = lax.dot_general(dz[t + e], w_blk, (((1,), (1,)), ((), ())), preferred_element_type=F32)
+            q[e] = (d_act * gp[gs]).astype(BF16)
+        for e in range(2):
+            acc = jnp.dot(xT[...], q[e], preferred_element_type=F32)
+            row = inv[t + e][0:1, :]
+            hb[hs, 0, t + e] = (acc[:, :128] * row).astype(BF16)
+            hb[hs, 1, t + e] = (acc[:, 128:] * row).astype(BF16)
+
+    def compute(k, third):
+        @pl.when(k < nchunk)
+        def _():
+            @pl.when((third == 0) & (k >= 2))
             def _():
-                gp_load(fb + 1).start()
-        w_blk = w2[pl.ds(pl.multiple_of(fb * 256, 256), 256), :]
-        for t in range(4 * half, 4 + 2 * half):
-            d_act = lax.dot_general(dz[t], w_blk, (((1,), (1,)), ((), ())), preferred_element_type=F32)
-            q[t % 2] = (d_act * gp[gs]).astype(BF16)
-            acc = jnp.dot(xT[...], q[t % 2], preferred_element_type=F32)
-            row = inv[t][0:1, :]
-            hb[hs, 0, t] = (acc[:, :128] * row).astype(BF16)
-            hb[hs, 1, t] = (acc[:, 128:] * row).astype(BF16)
-
-    def compute(k, half):
-        @pl.when(k < nchunk)
-        def _():
-            if half == 0:
-                @pl.when(k >= 2)
-                def _():
-                    half_copy(k, 0).wait_send()
-                    half_copy(k, 1).wait_send()
+                for i in range(3):
+                    pair_copy(k, i).wait_send()
 
             @pl.when(lax.rem(k, 2) == 0)
             def _():
-                compute_out(k, half)
+                compute_out(k, third)
 
             @pl.when(lax.rem(k, 2) == 1)
             def _():
-                compute_in(k, half)
-            half_copy(k, half).start()
-
-    def at(k, fn):
-        @pl.when((k >= 0) & (k < nchunk))
+                compute_in(k, third)
+            pair_copy(k, third).start()
+
+    def at(third, want, k, fn):
+        @pl.when((third == want) & (k >= 0) & (k < nchunk))
         def _():
             fn(k)
 
-    def slot(kk, _):
-        at(kk - 3, functools.partial(relay, 0))
-        at(kk - 6, functools.partial(relay, 1))
-        at(kk - 9, functools.partial(relay, 2))
-        compute(kk, 0)
-        at(kk - 1, merge)
-        at(kk - 4, functools.partial(close, 0))
-        at(kk - 7, functools.partial(close, 1))
-        at(kk - 10, functools.partial(close, 2))
-        compute(kk, 1)
+    def step(u, _):
+        kk, third = lax.div(u, 3), lax.rem(u, 3)
+        at(third, 0, kk - 3, functools.partial(relay, 0))
+        at(third, 0, kk - 6, functools.partial(relay, 1))
+        at(third, 0, kk - 9, functools.partial(relay, 2))
+        at(third, 1, kk - 1, merge)
+        at(third, 1, kk - 4, functools.partial(close, 0))
+        at(third, 1, kk - 7, functools.partial(close, 1))
+        at(third, 1, kk - 10, functools.partial(close, 2))
+        compute(kk, third)
         return 0
-    lax.fori_loop(0, nchunk + 10, slot, 0)
+    lax.fori_loop(0, 3 * (nchunk + 10), step, 0)
 
     for i in range(DEPTH):
         for p in range(3):
             drain_sends(p, i)
     for k in (nchunk - 2, nchunk - 1):
-        half_copy(k, 0).wait_send()
-        half_copy(k, 1).wait_send()
+        for third in range(3):
+            pair_copy(k, third).wait_send()
+
+    swap = pltpu.make_async_remote_copy(
+        src_ref=shard, dst_ref=other, send_sem=gs_sem, recv_sem=gr_sem,
+        device_id=(partner,), device_id_type=MESH)
+    swap.start()
 
     pairs = [(t, s) for t in range(T) for s in range(t, T)]
 
@@ -326,38 +337,39 @@
         gram = jnp.where(hit, val, gram)
     gram = all_reduce(4, gram)
 
-    diag = jnp.where(row_id == col_id, gram, 0.0)
-    scale = jnp.sum(jnp.sum(diag, axis=0, keepdims=True), axis=1, keepdims=True) / T
-    w_row = jnp.where(col_id[0:1, :] < T, jnp.full((1, 128), 1.0 / T, F32), 0.0)
-    w_col = jnp.where(row_id[:, 0:1] < T, jnp.full((8, 1), 1.0 / T, F32), 0.0)
-
-    def solver(_, carry):
-        wr, wc = carry
-        pull_c = jnp.sum(gram * wr, axis=1, keepdims=True)
-        pull_r = jnp.sum(gram * wc, axis=0, keepdims=True)
-        rc = wc * jnp.exp(-pull_c / scale)
-        rr = wr * jnp.exp(-pull_r / scale)
-        return rr / jnp.sum(rr, axis=1, keepdims=True), rc / jnp.sum(rc, axis=0, keepdims=True)
-    w_row, w_col = lax.fori_loop(0, SOLVER_STEPS, solver, (w_row, w_col))
-    alpha_ref[...] = jnp.broadcast_to(w_row, (8, 128))
-
-    alphas = [jnp.broadcast_to(w_col[t:t + 1, :], (8, 128)) for t in range(T)]
+    def entry(t, s):
+        return jnp.broadcast_to(gram[t:t + 1, s:s + 1], (8, 128))
+    upper = {(t, s): entry(t, s) for t, s in pairs}
+    scale = upper[0, 0]
+    for t in range(1, T):
+        scale = scale + upper[t, t]
+    scale = scale / T
+
+    def tree(v):
+        return (v[0] + v[1]) + (v[2] + v[3]) + (v[4] + v[5])
+
+    def solver(_, w):
+        raised = []
+        for t in range(T):
+            pull = tree([upper[min(t, s), max(t, s)] * w[s] for s in range(T)])
+            raised.append(w[t] * jnp.exp(-pull / scale))
+        tot = tree(raised)
+        return tuple(r / tot for r in raised)
+    alphas = lax.fori_loop(0, SOLVER_STEPS, solver, tuple(jnp.full((8, 128), 1.0 / T, F32) for _ in range(T)))
+    packed = jnp.zeros((8, 128), F32)
+    for t in range(T):
+        packed = jnp.where(col_id == t, alphas[t], packed)
+    alpha_ref[...] = packed
+    swap.wait()
 
     def combine(k, _):
-        tot = alphas[0] * shard[0, k]
-        for t in range(1, T):
-            tot = tot + alphas[t] * shard[t, k]
-        gb[core, k] = tot
+        for ref, who in ((shard, core), (other, 1 - core)):
+            gb[who, k] = tree([alphas[t] * ref[t, k] for t in range(T)])
         return 0
     lax.fori_loop(0, nchunk, combine, 0)
-    swap = pltpu.make_async_remote_copy(
-        src_ref=gb.at[core], dst_ref=gb.at[core], send_sem=gs_sem, recv_sem=gr_sem,
-        device_id=(partner,), device_id_type=MESH)
-    swap.start()
-    swap.wait()
     for h in range(2):
         for fb in range(nfb):
-            tile = gb[h, 2 * fb + 1]
+            tile = gb[h, 2 * ((fb + 2) % nfb) + 1]
             rows = jnp.where(core == 0, tile[0:4], tile[4:8])
             for r in range(4):
                 o = r * 2 * nfb + 2 * fb + h
@@ -369,7 +381,7 @@
                 out2_ref[o:o + 1, :] = tile[r:r + 1]
 
 
-def reduce_and_solve(code, ht3, ht24, x_loc, w_in, w_out):
+def reduce_and_solve(lab, mask, ht24, x_loc, w_in, w_out):
     any_spec = pl.BlockSpec(memory_space=pl.ANY)
     vm = pl.BlockSpec(memory_space=pltpu.VMEM)
     V = pltpu.VMEM
@@ -383,27 +395,25 @@
         out_specs=[vm] * 3 + [any_spec],
         scratch_shapes=[
             V((64, 2, 16, 2048), BF16), V((512, 2048), BF16), V((T, 2048, 512), BF16), V((2048, 512), BF16),
-            V((2, 2048, 256), F32), V((2, 2048, 256), BF16), V((T, 128, 512), BF16), V((T, 8, 128), F32),
+            V((2, 2048, 256), F32), V((2, 2048, 256), BF16), V((T, 128, 512), BF16),
+            V((128, 2048), F32), V((384, 512), BF16), V((T, 16, 8, 128), F32), V((T, 8, 128), F32),
             V((2, 2, T, 512, 128), BF16), V((XRING, T, 512, 128), BF16),
             V((DEPTH, T, 4, 4, 4, 8, 128), F32), V((DEPTH, T, 4, 4, 8, 128), F32), V((DEPTH, T, 4, 8, 128), F32),
             V((RING, 3, T, 4, 4, 8, 128), F32), V((RING, 3, T, 4, 8, 128), F32), V((RING, 3, T, 8, 128), F32),
             V((T, 16, 8, 128), F32), V((2, 16, 8, 128), F32), V((8, 8, 128), F32), V((8, 4, 8, 128), F32),
-            DS((4,)), DS((2,)), DS((2, 2)), DS((XRING, 2)), DS((3, DEPTH)), DS((3, 2, RING)),
+            DS((4,)), DS((2,)), DS((2, 3)), DS((XRING, 3)), DS((3, DEPTH)), DS((3, 2, RING)),
             DS((8,)), DS((8,)), DS, DS,
         ],
         compiler_params=pltpu.CompilerParams(collective_id=0, has_side_effects=True, vmem_limit_bytes=67043328),
-    )(code, ht3, ht24, x_loc, w_in, w_out)
+    )(lab, mask, ht24, x_loc, w_in, w_out)
 
 
 def solution(mesh):
     def local_step(x_loc, w_in, w_out, task_heads, lab_loc, mask_loc):
-        code = jnp.where(mask_loc > 0, lab_loc, -1).astype(F32)
-        code = jnp.pad(code, ((0, 122), (0, 0)), constant_values=-1.0)
         by_class = task_heads.transpose(2, 0, 1)
-        ht3 = jnp.pad(by_class, ((0, 0), (0, 122), (0, 0))).reshape(384, 512)
         ht24 = jnp.pad(by_class, ((0, 0), (0, 2), (0, 0))).reshape(24, 512)
         ht24 = jnp.pad(ht24, ((0, 104), (0, 0)))
-        alpha, g_in, g_out, _ = reduce_and_solve(code, ht3, ht24, x_loc, w_in, w_out)
+        alpha, g_in, g_out, _ = reduce_and_solve(lab_loc, mask_loc, ht24, x_loc, w_in, w_out)
         return alpha[0, :6], g_in.reshape(-1), g_out.reshape(-1)
 
     return jax.shard_map(local_step, mesh=mesh, in_specs=(P("data", None), P(), P(), P(), P(None, "data"), P(None, "data")), out_specs=(P(), P("data"), P("data")), check_vma=False)

time: 202 us -> 179 us (0.89)
  Pallas kernels: 193 us -> 171 us
    pallas_call x1, Pallas kernels: 193 us -> 171 us  [reduce_and_solve(): pl.pallas_call(kernel, name='grads_rs', out_shape=[jax.ShapeDtypeStruct(s...]
where the time goes in v4:
time: 179 us; the launch traced here: 177 us
  Pallas kernels  171 us (96%)
  local copies, waits for them, and re-layouts  5.36 us (3%)
    pallas_call x1, Pallas kernels, reduce_and_solve(): pl.pallas_call(kernel, name='grads_rs', out_shape=[jax.ShapeDtypeStruct(s...  171 us

profile of v4, /device:TPU:1, one launch (start us, length us, event | category | flops | bytes accessed | tf_op | source)
XLA Modules:
  0.0 177.1 jit_solution(8654893892971639360)
XLA Ops:
  0.6 0.7 copy.10
  1.4 0.7 pad.9.ht24_ref
  2.0 171.1 %grads_rs.1 = (f32[8,128]{1,0:T(8,128)}, f32[64,128]{1,0:T(8,128)}, f32[64,128]{1,0:T(8,128)}, f32[8,2048,256]{2,1,0:T(8,128)}) custom-call(s32[6,2048]{1,0:T(8,128)} %lab_ref.1, s32[6,2048]{1,0:T(8,128)} %mask_ref.1, bf16[128,512]{1,0:T(8,128)(2,1)} %pad.9.ht24_ref, bf16[2048,512]{1,0:T(8,128)(2,1)} %x_hbm.1, bf16[512,2048]{1,0:T(8,128)(2,1)} %w1_hbm.1, ...), custom_call_target="tpu_custom_call" | custom-call | tf_op jit(solution)/shard_map/grads_rs/pallas_call | solution.py:390
  173.1 1.2 slice_bitcast_fusion
  174.3 1.4 copy.13
  175.7 1.4 copy.14
  (1 shorter events, 0.0 us)

commit v5 on v4

--- a/solution.py
+++ b/solution.py
@@ -9,6 +9,8 @@
 
 SOLVER_STEPS = 20
 T = 6
+NT = (((1,), (1,)), ((), ()))
+TILE = (8, 128)
 MESH = pl.DeviceIdType.MESH
 STRIDES = (32, 8, 2)
 RING, DEPTH, XRING = 8, 4, 3
@@ -20,7 +22,7 @@
 
 
 def kernel(lab_ref, mask_ref, ht24_ref, x_hbm, w1_hbm, w2_hbm,
-           alpha_ref, out1_ref, out2_ref, gp_hbm,
+           out_ref, gp_hbm,
            aT, xT, dz, w2, gp, q, hbig, code_ref, ht3_ref, other, inv, hb, xr, dbuf, ebuf, fbuf, r1, r2, r3, shard, gb, ar_s, ar_r,
            ld_sem, gp_sem, xs_sem, xr_sem, s_sem, r_sem, ars_sem, arr_sem, gs_sem, gr_sem):
     nchunk, nfb = 16, 8
@@ -49,42 +51,36 @@
         return pltpu.make_async_copy(gp.at[lax.rem(fb, 2)], gp_hbm.at[fb], gp_sem.at[lax.rem(fb, 2)])
 
     barrier = pltpu.get_barrier_semaphore()
-    peers = [(partner,)] + [nb(d, s) for d in range(3) for s in (1, -1, 2)]
+    plane = 4 * coord[1] + coord[2]
+    column = 2 * coord[0] + core
+    plane_peers = [(nb(1, dy)[0] + nb(2, dx)[0] - me,) for dy in range(4) for dx in range(4) if dy or dx]
+    column_peers = [(nb(0, dz_)[0] + dc * (partner - me),) for dz_ in range(4) for dc in range(2) if dz_ or dc]
+    peers = plane_peers + column_peers
     for p in peers:
         pl.semaphore_signal(barrier, inc=1, device_id=p, device_id_type=MESH)
-    pl.semaphore_wait(barrier, 10)
-
-    def ar_core(base):
-        return pltpu.make_async_remote_copy(
-            src_ref=ar_s.at[base], dst_ref=ar_r.at[base, 0], send_sem=ars_sem.at[base], recv_sem=arr_sem.at[base],
-            device_id=(partner,), device_id_type=MESH)
+    pl.semaphore_wait(barrier, 22)
 
     def ar_start(base, stage, val):
         s = base + stage
         ar_s[s] = val
-        if stage == 0:
-            ar_core(base).start()
-            return
-        dim = stage - 1
-        for step in (2, 1, 3):
+        for p in (plane_peers, column_peers)[stage]:
             pltpu.make_async_remote_copy(
-                src_ref=ar_s.at[s], dst_ref=ar_r.at[s, coord[dim]], send_sem=ars_sem.at[s], recv_sem=arr_sem.at[s],
-                device_id=nb(dim, step), device_id_type=MESH).start()
+                src_ref=ar_s.at[s], dst_ref=ar_r.at[s, (plane, column)[stage]], send_sem=ars_sem.at[s], recv_sem=arr_sem.at[s],
+                device_id=p, device_id_type=MESH).start()
 
     def ar_finish(base, stage):
         s = base + stage
-        if stage == 0:
-            ar_core(base).wait()
-            return ar_s[s] + ar_r[s, 0]
-        three = ar_r.at[s, pl.ds(0, 3)]
-        pltpu.make_async_copy(three, three, arr_sem.at[s]).wait()
-        pltpu.make_async_copy(three, three, ars_sem.at[s]).wait()
-        u = coord[stage - 1]
-        part = [jnp.where(u == i, ar_s[s], ar_r[s, i]) for i in range(4)]
-        return (part[0] + part[1]) + (part[2] + part[3])
+        n = (16, 8)[stage]
+        rest = ar_r.at[s, pl.ds(0, n - 1)]
+        pltpu.make_async_copy(rest, rest, arr_sem.at[s]).wait()
+        pltpu.make_async_copy(rest, rest, ars_sem.at[s]).wait()
+        part = [jnp.where((plane, column)[stage] == i, ar_s[s], ar_r[s, i]) for i in range(n)]
+        while len(part) > 1:
+            part = [a + b for a, b in zip(part[::2], part[1::2])]
+        return part[0]
 
     def all_reduce(base, val):
-        for stage in range(4):
+        for stage in range(2):
             ar_start(base, stage, val)
             val = ar_finish(base, stage)
         return val
@@ -92,17 +88,16 @@
     code_ref[...] = jnp.full(code_ref.shape, -1.0, F32)
     code_ref[0:T, :] = jnp.where(mask_ref[...] > 0, lab_ref[...], -1).astype(F32)
     cnt = jnp.sum((code_ref[0:8, :] >= 0).astype(F32), axis=1, keepdims=True)
-    ar_start(0, 0, jnp.broadcast_to(cnt, (8, 128)))
+    ar_start(0, 0, jnp.broadcast_to(cnt, TILE))
     for c in x_loads + [w1_load]:
         c.wait()
     K0, K1 = 0.7978845608028654, 0.044715
 
     def hidden(fb, _):
         cols = pl.ds(pl.multiple_of(fb * 256, 256), 256)
-        for stage in range(1, 4):
-            @pl.when(fb == 2 * stage)
-            def _():
-                ar_start(0, stage, ar_finish(0, stage - 1))
+        @pl.when(fb == 3)
+        def _():
+            ar_start(0, 1, ar_finish(0, 0))
 
         @pl.when(fb >= 2)
         def _():
@@ -114,8 +109,9 @@
             p2 = p * p
             th = jnp.tanh(p * (K0 + (K0 * K1) * p2))
             cdf = 0.5 + 0.5 * th
-            act = (p * cdf).astype(BF16)
-            gp[lax.rem(fb, 2), rows, :] = cdf + (0.5 - 0.5 * (th * th)) * (p * (K0 + (3 * K0 * K1) * p2))
+            wide = p * cdf
+            act = wide.astype(BF16)
+            gp[lax.rem(fb, 2), rows, :] = cdf + (wide * (1.0 - cdf)) * (2 * K0 + (6 * K0 * K1) * p2)
             dz[lax.div(fb, 2), rows, pl.ds(pl.multiple_of(lax.rem(fb, 2) * 256, 256), 256)] = act
             aT[pl.ds(fb * 8, 8), :, :, rows] = act.T.reshape(8, 2, 16, 512)
 
@@ -125,9 +121,9 @@
         return 0
     lax.fori_loop(0, nfb, hidden, 0)
 
-    inv_all = 1.0 / jnp.maximum(ar_finish(0, 3), 1.0)
+    inv_all = 1.0 / jnp.maximum(ar_finish(0, 1), 1.0)
     for t in range(T):
-        inv[t] = jnp.broadcast_to(inv_all[t:t + 1, :], (8, 128))
+        inv[t] = jnp.broadcast_to(inv_all[t:t + 1, :], TILE)
 
     heads = ht24_ref[...].astype(F32)
     for c in range(3):
@@ -144,7 +140,7 @@
             z = z + jnp.dot(dz[j, rows, :], w2[512 * j:512 * j + 512, :], preferred_element_type=F32)
         x_t = jnp.concatenate([q[0, rows, :], q[1, rows, :]], axis=1)
         zb = (x_t.astype(F32) + z).astype(BF16)
-        logits = lax.dot_general(zb, ht3_ref[...], (((1,), (1,)), ((), ())), preferred_element_type=F32)
+        logits = lax.dot_general(zb, ht3_ref[...], NT, preferred_element_type=F32)
         ls = [logits[:, 128 * c:128 * c + 128] for c in range(3)]
         top = jnp.maximum(jnp.maximum(ls[0], ls[1]), ls[2])
         ex = [jnp.exp(v - top) for v in ls]
@@ -178,13 +174,19 @@
             send_sem=s_sem.at[p, d], recv_sem=r_sem.at[p, 0 if kind == 0 else 1, slot],
             device_id=nb(dim, step), device_id_type=MESH).start()
 
-    def open_phase(p, k):
-        for t in range(T):
+    def open_phase(p, k, tasks=tuple(range(T))):
+        for t in tasks:
             dim, sg = dims_of(p, t)
-            send(p, k, t, rel(dim, 2), 0, sg, dim)
-        for t in range(T):
+            send(p, k, t, rel(dim, 2), 0, jnp.where(k == nchunk - 1, 2, sg) if p == 2 else sg, dim)
+        for t in tasks:
             dim, sg = dims_of(p, t)
             send(p, k, t, rel(dim, -sg), 1, -sg, dim)
+        if p == 2:
+            @pl.when(k == nchunk - 1)
+            def _():
+                for t in tasks:
+                    dim, sg = dims_of(p, t)
+                    send(p, k, t, rel(dim, sg), 2, sg, dim)
 
     def relay(p, k):
         slot, d = lax.rem(k, RING), lax.rem(k, DEPTH)
@@ -206,6 +208,14 @@
             @pl.when(k >= DEPTH)
             def _():
                 drain_sends(p + 1, d)
+        else:
+            @pl.when(k == nchunk - 1)
+            def _():
+                far = r3.at[slot, 0]
+                pltpu.make_async_copy(far, far, r_sem.at[p, 0, slot]).wait()
+                for t in range(T):
+                    mine = coord[dims_of(p, t)[0]]
+                    fbuf[d, t, mine] = fbuf[d, t, mine] + r3[slot, 0, t]
         for t in range(T):
             dim, _ = dims_of(p, t)
             out = srcs[p][d, t, coord[dim]] + recvs[p][slot, 1, t] + recvs[p][slot, 2, t]
@@ -223,23 +233,22 @@
             send_sem=xs_sem.at[hs, third], recv_sem=xr_sem.at[xs, third],
             device_id=(partner,), device_id_type=MESH)
 
-    def merge(k):
+    def merge(pair, k):
         d, hs, xs = lax.rem(k, DEPTH), lax.rem(k, 2), lax.rem(k, XRING)
-        for third in range(3):
-            pair_copy(k, third).wait_recv()
-
-        @pl.when(k >= DEPTH)
-        def _():
-            drain_sends(0, d)
-        for t in range(T):
-            for pair in range(32):
-                rows = slice(16 * pair, 16 * pair + 16)
+        pair_copy(k, pair).wait_recv()
+        if pair == 0:
+            @pl.when(k >= DEPTH)
+            def _():
+                drain_sends(0, d)
+        for t in (2 * pair, 2 * pair + 1):
+            for two in range(32):
+                rows = slice(16 * two, 16 * two + 16)
                 s = hb[hs, core, t, rows, :].astype(F32) + xr[xs, t, rows, :].astype(F32)
                 for e in range(2):
-                    i = 2 * pair + e
+                    i = 2 * two + e
                     a, b, c = perm(t % 3, i // 16, (i // 4) % 4, i % 4)
                     dbuf[d, t, a, b, c] = s[8 * e:8 * e + 8]
-        open_phase(0, k)
+        open_phase(0, k, (2 * pair, 2 * pair + 1))
 
     def compute_out(k, third):
         j = lax.div(k, 2)
@@ -267,7 +276,7 @@
             gp_load(lax.rem(fb + 1, nfb)).start()
         w_blk = w2[pl.ds(pl.multiple_of(fb * 256, 256), 256), :]
         for e in range(2):
-            d_act = lax.dot_general(dz[t + e], w_blk, (((1,), (1,)), ((), ())), preferred_element_type=F32)
+            d_act = lax.dot_general(dz[t + e], w_blk, NT, preferred_element_type=F32)
             q[e] = (d_act * gp[gs]).astype(BF16)
         for e in range(2):
             acc = jnp.dot(xT[...], q[e], preferred_element_type=F32)
@@ -292,8 +301,14 @@
                 compute_in(k, third)
             pair_copy(k, third).start()
 
-    def at(third, want, k, fn):
-        @pl.when((third == want) & (k >= 0) & (k < nchunk))
+    last = nchunk - 1
+
+    def merge_all(k):
+        for pair in range(3):
+            merge(pair, k)
+
+    def at(third, want, k, fn, lo=0, hi=nchunk):
+        @pl.when((third == want) & (k >= lo) & (k < hi))
         def _():
             fn(k)
 
@@ -301,8 +316,11 @@
         kk, third = lax.div(u, 3), lax.rem(u, 3)
         at(third, 0, kk - 3, functools.partial(relay, 0))
         at(third, 0, kk - 6, functools.partial(relay, 1))
-        at(third, 0, kk - 9, functools.partial(relay, 2))
-        at(third, 1, kk - 1, merge)
+        at(third, 0, kk - 9, functools.partial(relay, 2), hi=last)
+        at(third, 1, kk - 1, merge_all, hi=last)
+        at(third, 2, kk, functools.partial(merge, 0), lo=last)
+        at(third, 0, kk - 1, functools.partial(merge, 1), lo=last)
+        at(third, 1, kk - 1, functools.partial(merge, 2), lo=last)
         at(third, 1, kk - 4, functools.partial(close, 0))
         at(third, 1, kk - 7, functools.partial(close, 1))
         at(third, 1, kk - 10, functools.partial(close, 2))
@@ -327,18 +345,18 @@
     def gram_step(k, accs):
         rows = [shard[t, k] for t in range(T)]
         return tuple(acc + rows[t] * rows[s] for acc, (t, s) in zip(accs, pairs))
-    accs = lax.fori_loop(0, nchunk, gram_step, tuple(jnp.zeros((8, 128), F32) for _ in pairs))
-    row_id = lax.broadcasted_iota(jnp.int32, (8, 128), 0)
-    col_id = lax.broadcasted_iota(jnp.int32, (8, 128), 1)
-    gram = jnp.zeros((8, 128), F32)
+    accs = lax.fori_loop(0, nchunk, gram_step, tuple(jnp.zeros(TILE, F32) for _ in pairs))
+    row_id = lax.broadcasted_iota(jnp.int32, TILE, 0)
+    col_id = lax.broadcasted_iota(jnp.int32, TILE, 1)
+    gram = jnp.zeros(TILE, F32)
     for acc, (t, s) in zip(accs, pairs):
         val = jnp.sum(jnp.sum(acc, axis=0, keepdims=True), axis=1, keepdims=True)
         hit = ((row_id == t) & (col_id == s)) | ((row_id == s) & (col_id == t))
         gram = jnp.where(hit, val, gram)
-    gram = all_reduce(4, gram)
+    gram = all_reduce(2, gram)
 
     def entry(t, s):
-        return jnp.broadcast_to(gram[t:t + 1, s:s + 1], (8, 128))
+        return jnp.broadcast_to(gram[t:t + 1, s:s + 1], TILE)
     upper = {(t, s): entry(t, s) for t, s in pairs}
     scale = upper[0, 0]
     for t in range(1, T):
@@ -355,11 +373,11 @@
             raised.append(w[t] * jnp.exp(-pull / scale))
         tot = tree(raised)
         return tuple(r / tot for r in raised)
-    alphas = lax.fori_loop(0, SOLVER_STEPS, solver, tuple(jnp.full((8, 128), 1.0 / T, F32) for _ in range(T)))
-    packed = jnp.zeros((8, 128), F32)
+    alphas = lax.fori_loop(0, SOLVER_STEPS, solver, tuple(jnp.full(TILE, 1.0 / T, F32) for _ in range(T)))
+    packed = jnp.zeros(TILE, F32)
     for t in range(T):
         packed = jnp.where(col_id == t, alphas[t], packed)
-    alpha_ref[...] = packed
+    out_ref[128:136, :] = packed
     swap.wait()
 
     def combine(k, _):
@@ -373,12 +391,12 @@
             rows = jnp.where(core == 0, tile[0:4], tile[4:8])
             for r in range(4):
                 o = r * 2 * nfb + 2 * fb + h
-                out1_ref[o:o + 1, :] = rows[r:r + 1]
+                out_ref[o:o + 1, :] = rows[r:r + 1]
         for cb in range(4):
             tile = gb[h, 2 * (4 * core + cb)]
             for r in range(8):
                 o = (8 * h + r) * 4 + cb
-                out2_ref[o:o + 1, :] = tile[r:r + 1]
+                out_ref[64 + o:65 + o, :] = tile[r:r + 1]
 
 
 def reduce_and_solve(lab, mask, ht24, x_loc, w_in, w_out):
@@ -386,23 +404,23 @@
     vm = pl.BlockSpec(memory_space=pltpu.VMEM)
     V = pltpu.VMEM
     DS = pltpu.SemaphoreType.DMA
-    shapes = [(8, 128), (64, 128), (64, 128), (8, 2048, 256)]
+    shapes = [(136, 128), (8, 2048, 256)]
     return pl.pallas_call(
         kernel,
         name="grads_rs",
         out_shape=[jax.ShapeDtypeStruct(s, F32) for s in shapes],
         in_specs=[vm] * 3 + [any_spec] * 3,
-        out_specs=[vm] * 3 + [any_spec],
+        out_specs=[vm, any_spec],
         scratch_shapes=[
             V((64, 2, 16, 2048), BF16), V((512, 2048), BF16), V((T, 2048, 512), BF16), V((2048, 512), BF16),
             V((2, 2048, 256), F32), V((2, 2048, 256), BF16), V((T, 128, 512), BF16),
-            V((128, 2048), F32), V((384, 512), BF16), V((T, 16, 8, 128), F32), V((T, 8, 128), F32),
+            V((128, 2048), F32), V((384, 512), BF16), V((T, 16, *TILE), F32), V((T, *TILE), F32),
             V((2, 2, T, 512, 128), BF16), V((XRING, T, 512, 128), BF16),
-            V((DEPTH, T, 4, 4, 4, 8, 128), F32), V((DEPTH, T, 4, 4, 8, 128), F32), V((DEPTH, T, 4, 8, 128), F32),
-            V((RING, 3, T, 4, 4, 8, 128), F32), V((RING, 3, T, 4, 8, 128), F32), V((RING, 3, T, 8, 128), F32),
-            V((T, 16, 8, 128), F32), V((2, 16, 8, 128), F32), V((8, 8, 128), F32), V((8, 4, 8, 128), F32),
+            *[V((DEPTH, T) + (4,) * n + TILE, F32) for n in (3, 2, 1)],
+            *[V((RING, 3, T) + (4,) * n + TILE, F32) for n in (2, 1, 0)],
+            V((T, 16, *TILE), F32), V((2, 16, *TILE), F32), V((4, *TILE), F32), V((4, 16, *TILE), F32),
             DS((4,)), DS((2,)), DS((2, 3)), DS((XRING, 3)), DS((3, DEPTH)), DS((3, 2, RING)),
-            DS((8,)), DS((8,)), DS, DS,
+            DS((4,)), DS((4,)), DS, DS,
         ],
         compiler_params=pltpu.CompilerParams(collective_id=0, has_side_effects=True, vmem_limit_bytes=67043328),
     )(lab, mask, ht24, x_loc, w_in, w_out)
@@ -413,7 +431,7 @@
         by_class = task_heads.transpose(2, 0, 1)
         ht24 = jnp.pad(by_class, ((0, 0), (0, 2), (0, 0))).reshape(24, 512)
         ht24 = jnp.pad(ht24, ((0, 104), (0, 0)))
-        alpha, g_in, g_out, _ = reduce_and_solve(lab_loc, mask_loc, ht24, x_loc, w_in, w_out)
-        return alpha[0, :6], g_in.reshape(-1), g_out.reshape(-1)
+        out, _ = reduce_and_solve(lab_loc, mask_loc, ht24, x_loc, w_in, w_out)
+        return out[128, :T], out[:64].reshape(-1), out[64:128].reshape(-1)
 
     return jax.shard_map(local_step, mesh=mesh, in_specs=(P("data", None), P(), P(), P(), P(None, "data"), P(None, "data")), out_specs=(P(), P("data"), P("data")), check_vma=False)

time: 179 us -> 174 us (0.972); the launches traced: 177 us -> 174 us
  Pallas kernels: 171 us -> 169 us
    unnamed x3 -> x1, local copies, waits for them, and re-layouts: 3.49 us -> 0.75 us
where the time goes in v5:
time: 174 us
  Pallas kernels  169 us (97%)
  local copies, waits for them, and re-layouts  4.01 us (2%)
    pallas_call x1, Pallas kernels, reduce_and_solve(): pl.pallas_call(kernel, name='grads_rs', out_shape=[jax.ShapeDtypeStruct(s...  169 us

profile of v5, /device:TPU:1, one launch (start us, length us, event | category | flops | bytes accessed | tf_op | source)
XLA Modules:
  0.0 174.0 jit_solution(11812833313084005644)
XLA Ops:
  0.6 0.7 copy.10
  1.4 0.7 pad.9.ht24_ref
  2.0 169.4 %grads_rs.1 = (f32[136,128]{1,0:T(8,128)}, f32[8,2048,256]{2,1,0:T(8,128)}) custom-call(s32[6,2048]{1,0:T(8,128)} %lab_ref.1, s32[6,2048]{1,0:T(8,128)} %mask_ref.1, bf16[128,512]{1,0:T(8,128)(2,1)} %pad.9.ht24_ref, bf16[2048,512]{1,0:T(8,128)(2,1)} %x_hbm.1, bf16[512,2048]{1,0:T(8,128)(2,1)} %w1_hbm.1, bf16[2048,512]{1,0:T(8,128)(2,1)} %w2_hbm.1), custom_call_target="tpu_custom_call" | custom-call | tf_op jit(solution)/shard_map/grads_rs/pallas_call | solution.py:408
  171.4 1.2 slice_bitcast_fusion.2
  172.6 1.4 slice_bitcast_fusion
  (1 shorter events, 0.0 us)
